TPU v7x, 32 devices: a whole 2x2x4 slice. The times are simulated.
32 devices in a mesh: rows: 8 (over z, y), rep: 4 (over x, core).
Axes of the slice: x: 2, y: 2, z: 4, core: 2. Of those that a mesh axis runs over, the one named last changes fastest.
Arguments:
- field_in: bfloat16 [64, 384, 256], P('rows'), may hold values from -6 to 6
- left_factors: bfloat16 [1024, 384, 64], P(('rows', 'rep')), may hold values from -0.3125 to 0.3125
- right_factors: bfloat16 [1024, 384, 64], P(('rows', 'rep')), may hold values from -0.1875 to 0.1875
- block_ranks: int32 [1024], P(('rows', 'rep')), may hold values from 8 to 64
- row_cluster: int32 [1024], P(('rows', 'rep')), may hold values from 0 to 7
- col_owner: int32 [1024, 1], P(('rows', 'rep')), may hold values from 0 to 7; in each aligned block of 32 rows (0 to 31, 32 to 63, ...) at most 6 rows name the same one
- col_cluster: int32 [1024], P(('rows', 'rep')), may hold values from 0 to 7
- near_blocks: bfloat16 [64, 3, 384, 384], P('rows', None, 'rep'), may hold values from -0.1875 to 0.1875
Outputs:
- result_field: float32 [64, 384, 256], P('rows')
Inputs may be any that keep to these rules, and one draw needn't show every extreme that they name: `col_owner`: among the 32 blocks of one device no owner is named more than once.
All inputs are finite; a program needn't handle non-finite values.
Results may differ from a plain program's by a relative error of at most 0.0029.
Values may be sent and summed in bfloat16 or wider, within the bound.
A program may use at most 128 MiB of HBM per device.

v0:
```python
import functools

import jax
import jax.numpy as jnp
from jax import lax
from jax.experimental import pallas as pl
from jax.experimental.pallas import tpu as pltpu
from jax.sharding import PartitionSpec as P

MESH = pl.DeviceIdType.MESH
PARTS = 2
BF16 = jnp.bfloat16
F32 = jnp.float32


def dot_rows(left, right):
    return lax.dot_general(left, right, (((0,), (0,)), ((), ())), preferred_element_type=F32)


def kernel(
    owners, reps, most, joint, tab, field, ut, vt, near, out,
    vsend, vrecv, vtr, csend, crecv, hnear, hfield, total, *rest,
):
    stages = reps.bit_length() - 1
    rsend, rrecv = rest[:stages], rest[stages:2 * stages]
    vs, vr, cs, cr, hs, hr, rs, rr, gs, gr = rest[2 * stages:2 * stages + 10]
    extras = rest[2 * stages + 10:]
    group = owners // 2 if joint else owners
    row, rep = lax.axis_index("rows"), lax.axis_index("rep")
    place_in = lax.rem(row, group)
    base = row - place_in
    blocks, rank, width = ut.shape
    clusters, _, columns = field.shape
    share = near.shape[2]
    part = columns // PARTS
    depth = most * rank
    peers = group - 1

    barrier = pltpu.get_barrier_semaphore()

    @pl.loop(1, owners)
    def _(d):
        pl.semaphore_signal(
            barrier, inc=1, device_id=(lax.rem(row + d, owners), rep), device_id_type=MESH
        )

    @pl.loop(1, reps)
    def _(d):
        pl.semaphore_signal(
            barrier, inc=1, device_id=(row, lax.rem(rep + d, reps)), device_id_type=MESH
        )

    def peer(d):
        return base + lax.rem(place_in + d, group)

    def turn(k):
        step = (k + 1) // 2
        return group // 2 + lax.rem(k, 2) * step - (1 - lax.rem(k, 2)) * step

    def v_copy(d):
        return pltpu.make_async_remote_copy(
            src_ref=vsend.at[d], dst_ref=vrecv.at[d], send_sem=vs.at[d], recv_sem=vr.at[d],
            device_id=(peer(d), rep), device_id_type=MESH,
        )

    def c_copy(h, d):
        return pltpu.make_async_remote_copy(
            src_ref=csend.at[h, d], dst_ref=crecv.at[h, d],
            send_sem=cs.at[h, d], recv_sem=cr.at[h, d],
            device_id=(peer(d), rep), device_id_type=MESH,
        )

    def pack(d, target, owner):
        for j in range(most):
            target[d, pl.ds(j * rank, rank), :] = vt[tab[0, owner * most + j]]

    def coeffs(d, target, owner):
        extra = csend.shape[2] - depth
        lines = lax.broadcasted_iota(jnp.int32, (extra, part), 0)
        marks = jnp.full((extra, part), clusters, jnp.int32)
        for j in range(most):
            slot = owner * most + j
            value = jnp.dot(ut[tab[0, slot]], field[tab[1, slot]], preferred_element_type=F32)
            kept = lax.broadcasted_iota(jnp.int32, (rank, columns), 0) < tab[2, slot]
            value = jnp.where(kept, value, 0.0).astype(BF16)
            for h in range(PARTS):
                target[h, d, pl.ds(j * rank, rank), :] = value[:, h * part:(h + 1) * part]
            marks = jnp.where(lines == j, tab[3, slot], marks)
        for h in range(PARTS):
            target[h, d, pl.ds(depth, extra), :] = marks.astype(F32).astype(BF16)

    my_rows = pl.ds(pl.multiple_of(rep * share, share), share)

    def halo_copies():
        made = []
        for side, cluster, offset, shift in ((0, clusters - 1, 2, 1), (1, 0, 0, owners - 1)):
            where = (lax.rem(row + shift, owners), rep)
            made.append(pltpu.make_async_remote_copy(
                src_ref=near.at[cluster, offset], dst_ref=hnear.at[side],
                send_sem=hs.at[2 * side], recv_sem=hr.at[2 * side],
                device_id=where, device_id_type=MESH,
            ))
            made.append(pltpu.make_async_remote_copy(
                src_ref=field.at[cluster, my_rows, :], dst_ref=hfield.at[side],
                send_sem=hs.at[2 * side + 1], recv_sem=hr.at[2 * side + 1],
                device_id=where, device_id_type=MESH,
            ))
        return made

    plan = []
    low, size = 0, clusters
    for t in range(stages):
        bit = lax.rem(rep // (1 << t), 2)
        half = size // 2
        partner = rep + (1 << t) * (1 - 2 * bit)
        plan.append((half, partner, low + bit * half, low + (1 - bit) * half))
        low, size = low + bit * half, half

    def labels_of(source, h, d):
        return jnp.concatenate(
            [
                jnp.broadcast_to(source[h, d, pl.ds(depth + j, 1), :].astype(F32), (rank, part))
                for j in range(most)
            ],
            axis=0,
        ).astype(BF16)

    def part_of(right, source, labels, h, d, c):
        label = jnp.asarray(c, jnp.int32).astype(F32).astype(BF16)
        picked = jnp.where(
            labels == label, source[h, d, pl.ds(0, depth), :], jnp.zeros((), BF16)
        )
        return jnp.dot(right[d], picked, preferred_element_type=F32)

    levels = []
    crossed = None
    if joint:
        count = stages + group.bit_length() - 1
        jsend, jrecv = extras[:count], extras[count:2 * count]
        fv, fvt, fc, ftot, xsend, xrecv, js, jr, xs, xr = extras[2 * count:]
        crossed = xrecv
        first = plan[0][2]
        away_base = owners // 2 - base
        for h in range(PARTS):
            kinds = [("c", t) for t in range(stages)]
            kinds += [("e", g) for g in range(group.bit_length() - 1)]
            if h % 2:
                kinds = [kinds[0], kinds[stages], *kinds[1:stages], *kinds[stages + 1:]]
            mine, free = 0, list(range(group.bit_length() - 1))
            start, size = 0, clusters
            rows = []
            for kind, t in kinds:
                if kind == "c":
                    half, partner, keep, away = plan[t]
                    who = (row, partner)
                    size = half
                    keep_at, away_at = (keep, half), (away, half)
                    start = keep
                    keep_es = away_es = (mine, list(free))
                else:
                    bit = lax.rem(place_in // (1 << t), 2)
                    who = (row + (1 << t) * (1 - 2 * bit), rep)
                    free.remove(t)
                    keep_es = (mine + bit * (1 << t), list(free))
                    away_es = (mine + (1 - bit) * (1 << t), list(free))
                    mine = keep_es[0]
                    keep_at = away_at = (start, size)
                rows.append((who, keep_es, keep_at, away_es, away_at))
            levels.append(rows)

    def each(es, span, body):
        offset, free = es
        combos = [0]
        for bit in free:
            combos = combos + [value + (1 << bit) for value in combos]
        for spot, combo in enumerate(combos):
            @pl.loop(0, span[1])
            def _(i):
                body(spot * span[1] + i, offset + combo, span[0] + i)

    def j_copy(h, t):
        return pltpu.make_async_remote_copy(
            src_ref=jsend[t].at[h], dst_ref=jrecv[t].at[h],
            send_sem=js.at[h, t], recv_sem=jr.at[h, t],
            device_id=levels[h][t][0], device_id_type=MESH,
        )

    def x_copy(h):
        return pltpu.make_async_remote_copy(
            src_ref=xsend.at[h], dst_ref=xrecv.at[h],
            send_sem=xs.at[h], recv_sem=xr.at[h],
            device_id=(away_base + place_in, rep), device_id_type=MESH,
        )

    def j_give(h, t):
        _, _, _, es, span = levels[h][t]

        def body(n, e, c):
            jsend[t][h, n] = ftot[h, e, c - first].astype(BF16)

        each(es, span, body)
        j_copy(h, t).start()

    def j_take(h, t):
        _, es, span, _, _ = levels[h][t]
        j_copy(h, t).wait_recv()

        def body(n, e, c):
            ftot[h, e, c - first] = ftot[h, e, c - first] + jrecv[t][h, n].astype(F32)

        each(es, span, body)

    def j_first(h):
        half, _, keep, away = plan[0]

        @pl.loop(0, group)
        def _(e):
            labels = labels_of(fc, h, e)

            @pl.loop(0, half)
            def _(i):
                jsend[0][h, e * half + i] = part_of(fvt, fc, labels, h, e, away + i).astype(BF16)

        j_copy(h, 0).start()

        @pl.loop(0, group)
        def _(e):
            labels = labels_of(fc, h, e)

            @pl.loop(0, half)
            def _(i):
                ftot[h, e, i] = part_of(fvt, fc, labels, h, e, keep + i)

    def j_last(h):
        j_take(h, count - 1)

        @pl.loop(0, plan[-1][0])
        def _(i):
            xsend[h, i] = ftot[h, place_in, plan[-1][2] + i - first].astype(BF16)

        x_copy(h).start()

    pl.semaphore_wait(barrier, owners + reps - 2)

    if joint:
        @pl.loop(0, group)
        def _(e):
            pack(e, fv, away_base + e)
            coeffs(e, fc, away_base + e)
            fvt[e] = fv[e].T

        for h in range(PARTS):
            j_first(h)

    @pl.loop(0, peers)
    def _(k):
        d = turn(k)
        pack(d, vsend, peer(d))
        v_copy(d).start()

    halos = halo_copies()
    for copy in halos:
        copy.start()

    @pl.loop(0, peers)
    def _(k):
        d = turn(k)
        coeffs(d, csend, peer(d))
        c_copy(0, d).start()

    for h in range(1, PARTS):
        @pl.loop(0, peers)
        def _(k):
            c_copy(h, turn(k)).start()

    if joint:
        for h in range(PARTS):
            j_take(h, 0)
            j_give(h, 1)

    pack(0, vrecv, row)
    coeffs(0, crecv, row)

    def put(c, value):
        for h in range(PARTS):
            total[h, c] = value[:, h * part:(h + 1) * part]

    def add(c, value):
        for h in range(PARTS):
            total[h, c] = total[h, c] + value[:, h * part:(h + 1) * part]

    @pl.loop(0, clusters)
    def _(c):
        put(c, dot_rows(near[c, 1], field[c, my_rows, :]))

    @pl.loop(0, clusters - 1)
    def _(c):
        add(c + 1, dot_rows(near[c, 2], field[c, my_rows, :]))
        add(c, dot_rows(near[c + 1, 0], field[c + 1, my_rows, :]))

    for copy in halos:
        copy.wait_recv()
    add(0, dot_rows(hnear[0], hfield[0]))
    add(clusters - 1, dot_rows(hnear[1], hfield[1]))

    def far(h, d):
        if h == 0:
            vtr[d] = vrecv[d].T
        labels = labels_of(crecv, h, d)

        @pl.loop(0, clusters)
        def _(c):
            total[h, c] = total[h, c] + part_of(vtr, crecv, labels, h, d, c)

    def far_span(h, first, last):
        @pl.loop(first, last)
        def _(k):
            d = turn(peers - 1 - k)
            if h == 0:
                v_copy(d).wait_recv()
            c_copy(h, d).wait_recv()
            far(h, d)

    def r_copy(h, t):
        return pltpu.make_async_remote_copy(
            src_ref=rsend[t].at[h], dst_ref=rrecv[t].at[h],
            send_sem=rs.at[h, t], recv_sem=rr.at[h, t],
            device_id=(row, plan[t][1]), device_id_type=MESH,
        )

    def g_copy(h, t):
        half, partner, keep, _ = plan[t]
        block = out.at[pl.ds(keep, half), :, pl.ds(h * part, part)]
        return pltpu.make_async_remote_copy(
            src_ref=block, dst_ref=block, send_sem=gs.at[h, t], recv_sem=gr.at[h, t],
            device_id=(row, partner), device_id_type=MESH,
        )

    def give(h, t):
        half, _, _, away = plan[t]

        @pl.loop(0, half)
        def _(i):
            rsend[t][h, i] = total[h, away + i].astype(rsend[t].dtype)

        r_copy(h, t).start()

    def take(h, t):
        half, _, keep, _ = plan[t]
        r_copy(h, t).wait_recv()

        @pl.loop(0, half)
        def _(i):
            value = total[h, keep + i] + rrecv[t][h, i].astype(F32)
            if t == stages - 1:
                if joint:
                    value = value + crossed[h, i].astype(F32)
                out[keep + i, :, pl.ds(h * part, part)] = value.astype(BF16)
            else:
                total[h, keep + i] = value

    def sequence(h):
        steps = [lambda: give(h, 0)]
        for t in range(stages):
            if t < stages - 1:
                steps.append(lambda t=t: (take(h, t), give(h, t + 1)))
            else:
                steps.append(lambda t=t: (take(h, t), g_copy(h, t).start()))
        for t in range(stages - 1, 0, -1):
            steps.append(lambda t=t: (g_copy(h, t).wait_recv(), g_copy(h, t - 1).start()))
        steps.append(lambda: g_copy(h, 0).wait_recv())
        return steps

    ahead, behind = sequence(0), sequence(1)
    far(0, 0)
    far_span(0, 0, peers)
    ahead[0]()
    for step in ahead[1:stages]:
        step()
    if joint:
        far(1, 0)
        far_span(1, 0, peers)
        for step in behind[:stages]:
            step()
        for t in range(1, count - 1):
            for h in range(PARTS):
                j_take(h, t)
                j_give(h, t + 1)
        for h in range(PARTS):
            j_last(h)
        for h in range(PARTS):
            x_copy(h).wait_recv()
            (ahead, behind)[h][stages]()
        for one, two in zip(ahead[stages + 1:], behind[stages + 1:]):
            one()
            two()
    else:
        middle = peers // 2
        far(1, 0)
        far_span(1, 0, middle)
        ahead[stages]()
        far_span(1, middle, peers)
        behind[0]()
        later = ahead[stages + 1:]
        for place, step in enumerate(behind[1:]):
            if place < len(later):
                later[place]()
            step()

    @pl.loop(1, group)
    def _(d):
        v_copy(d).wait_send()
        for h in range(PARTS):
            c_copy(h, d).wait_send()

    if joint:
        for h in range(PARTS):
            x_copy(h).wait_send()
            for t in range(count):
                j_copy(h, t).wait_send()

    for copy in halos:
        copy.wait_send()
    for h in range(PARTS):
        for t in range(stages):
            r_copy(h, t).wait_send()
            g_copy(h, t).wait_send()


def shards(
    field_in,
    left_factors,
    right_factors,
    block_ranks,
    row_cluster,
    col_owner,
    col_cluster,
    near_blocks,
):
    owners, reps = lax.axis_size("rows"), lax.axis_size("rep")
    blocks, width, rank = left_factors.shape
    clusters, _, columns = field_in.shape
    share = near_blocks.shape[2]
    most = 5 * blocks // (4 * owners) + 1
    part = columns // PARTS
    depth = most * rank
    tall = depth + -(-most // 16) * 16
    stages = reps.bit_length() - 1

    target = col_owner[:, 0]
    number = jnp.arange(blocks, dtype=jnp.int32)
    same = (target[:, None] == target[None, :]) & (number[None, :] < number[:, None])
    slot = target * most + jnp.sum(same.astype(jnp.int32), axis=1)
    held = slot[:, None] == jnp.arange(owners * most, dtype=jnp.int32)[None, :]
    facts = jnp.stack([number, row_cluster, block_ranks, col_cluster - clusters])
    tab = jnp.sum(jnp.where(held[None], facts[:, :, None], 0), axis=1)
    tab = tab + jnp.array([0, 0, 0, clusters], jnp.int32)[:, None]

    vmem = pl.BlockSpec(memory_space=pltpu.VMEM)
    dma = pltpu.SemaphoreType.DMA
    halves = [clusters >> (t + 1) for t in range(stages)]
    steps = [
        pltpu.VMEM((PARTS, half, width, part), BF16 if t else F32) for t, half in enumerate(halves)
    ]
    joint = owners * clusters * width * columns <= 2 ** 23 and owners >= 4
    group = owners // 2 if joint else owners
    more = []
    if joint:
        count = stages + group.bit_length() - 1
        hops = [
            pltpu.VMEM((PARTS, (group * clusters) >> (t + 1), width, part), BF16)
            for t in range(count)
        ]
        last = pltpu.VMEM((PARTS, halves[-1], width, part), BF16)
        more = [
            *hops,
            *hops,
            pltpu.VMEM((group, depth, width), BF16),
            pltpu.VMEM((group, width, depth), BF16),
            pltpu.VMEM((PARTS, group, tall, part), BF16),
            pltpu.VMEM((PARTS, group, halves[0], width, part), F32),
            last,
            last,
            dma((PARTS, count)),
            dma((PARTS, count)),
            dma((PARTS,)),
            dma((PARTS,)),
        ]
    gathered = pl.pallas_call(
        functools.partial(kernel, owners, reps, most, joint),
        out_shape=jax.ShapeDtypeStruct(field_in.shape, BF16),
        in_specs=[pl.BlockSpec(memory_space=pltpu.SMEM)] + [vmem] * 4,
        out_specs=vmem,
        scratch_shapes=[
            pltpu.VMEM((group, depth, width), BF16),
            pltpu.VMEM((group, depth, width), BF16),
            pltpu.VMEM((group, width, depth), BF16),
            pltpu.VMEM((PARTS, group, tall, part), BF16),
            pltpu.VMEM((PARTS, group, tall, part), BF16),
            pltpu.VMEM((2, share, width), BF16),
            pltpu.VMEM((2, share, columns), BF16),
            pltpu.VMEM((PARTS, clusters, width, part), F32),
            *steps,
            *steps,
            dma((group,)),
            dma((group,)),
            dma((PARTS, group)),
            dma((PARTS, group)),
            dma((4,)),
            dma((4,)),
            dma((PARTS, stages)),
            dma((PARTS, stages)),
            dma((PARTS, stages)),
            dma((PARTS, stages)),
            *more,
        ],
        compiler_params=pltpu.CompilerParams(
            collective_id=0, has_side_effects=True, vmem_limit_bytes=60 * 1024 * 1024
        ),
    )(
        tab,
        field_in,
        jnp.swapaxes(left_factors, 1, 2),
        jnp.swapaxes(right_factors, 1, 2),
        near_blocks,
    )
    return gathered.astype(F32)


def solution(mesh):
    in_specs = (
        P("rows", None, None),
        P(("rows", "rep"), None, None),
        P(("rows", "rep"), None, None),
        P(("rows", "rep")),
        P(("rows", "rep")),
        P(("rows", "rep"), None),
        P(("rows", "rep")),
        P("rows", None, "rep", None),
    )
    out_specs = P("rows", None, None)
    return jax.shard_map(shards, mesh=mesh, in_specs=in_specs, out_specs=out_specs, check_vma=False)
```

profile of v0, /device:TPU:0, one launch (start us, length us, event | category | flops | bytes accessed | tf_op | source)
XLA Modules:
  0.0 121.0 jit_solution(8086110327415685402)
XLA Ops:
  0.0 0.7 add_bitcast_fusion
  0.7 0.9 convert_reduce_fusion
  1.6 0.7 fusion.1
  2.2 0.7 pad_add_fusion
  2.9 0.1 iota_compare_fusion
  3.0 0.1 select_reduce_fusion
  3.1 1.3 %broadcast_add_fusion.tab = s32[4,48]{1,0:T(4,128)} fusion(s32[4,48]{1,0:T(4,128)S(1)} %select_reduce_fusion, s32[4]{0:T(128)} %constant.9.clone), kind=kLoop, calls=%fused_computation.6 | loop fusion | flops 192 | bytes 1552 | tf_op jit(solution)/shard_map/add | solution.py:457
  4.4 113.2 %shard_map.91 = bf16[8,384,256]{2,1,0:T(8,128)(2,1)} custom-call(s32[4,48]{1,0:T(4,128)} %broadcast_add_fusion.tab, bf16[8,384,256]{2,1,0:T(8,128)(2,1)} %field.1, bf16[32,64,384]{2,1,0:T(8,128)(2,1)} %bitcast.13, bf16[32,64,384]{2,1,0:T(8,128)(2,1)} %bitcast.14, bf16[8,3,96,384]{3,2,1,0:T(8,128)(2,1)} %near.1), custom_call_target="tpu_custom_call" | custom-call | tf_op jit(solution)/shard_map/pallas_call | solution.py:489
  117.6 3.4 %convert_element_type.7 = f32[8,384,256]{2,1,0:T(8,128)} convert(bf16[8,384,256]{2,1,0:T(8,128)(2,1)} %shard_map.91) | non-fusion elementwise | flops 786432 | bytes 4718592 | tf_op jit(solution)/shard_map/convert_element_type | solution.py:527
  (1 shorter events, 0.0 us)
where the time goes:
time: 121 us
  Pallas kernels  113 us (93%)
  other arithmetic  7.74 us (6%)
    pallas_call x1, Pallas kernels, shards(): pl.pallas_call(functools.partial(kernel, owners, reps, most, joint), out_...  113 us
    convert_element_type x1, other arithmetic, shards(): return gathered.astype(F32)  3.36 us

commit v1 on v0

v1 whole, which is shorter than its diff:
```python
import functools

import jax
import jax.numpy as jnp
from jax import lax
from jax.experimental import pallas as pl
from jax.experimental.pallas import tpu as pltpu
from jax.sharding import PartitionSpec as P

MESH = pl.DeviceIdType.MESH
PARTS = 2
BF16 = jnp.bfloat16
F32 = jnp.float32


def dot_rows(left, right):
    return lax.dot_general(left, right, (((0,), (0,)), ((), ())), preferred_element_type=F32)


def kernel(
    owners, reps, most, tab, field, ut, vt, near, out,
    vsend, vrecv, vtr, csend, crecv, hnear, hfield, total, *rest,
):
    stages = reps.bit_length() - 1
    rsend, rrecv = rest[:stages], rest[stages:2 * stages]
    vs, vr, cs, cr, hs, hr, rs, rr, gs, gr = rest[2 * stages:]
    group = owners
    row, rep = lax.axis_index("rows"), lax.axis_index("rep")
    place_in = lax.rem(row, group)
    base = row - place_in
    blocks, rank, width = ut.shape
    clusters, _, columns = field.shape
    share = near.shape[2]
    part = columns // PARTS
    depth = most * rank
    peers = group - 1

    barrier = pltpu.get_barrier_semaphore()

    @pl.loop(1, owners)
    def _(d):
        pl.semaphore_signal(
            barrier, inc=1, device_id=(lax.rem(row + d, owners), rep), device_id_type=MESH
        )

    @pl.loop(1, reps)
    def _(d):
        pl.semaphore_signal(
            barrier, inc=1, device_id=(row, lax.rem(rep + d, reps)), device_id_type=MESH
        )

    def peer(d):
        return base + lax.rem(place_in + d, group)

    def turn(k):
        step = (k + 1) // 2
        return group // 2 + lax.rem(k, 2) * step - (1 - lax.rem(k, 2)) * step

    def v_copy(d):
        return pltpu.make_async_remote_copy(
            src_ref=vsend.at[d], dst_ref=vrecv.at[d], send_sem=vs.at[d], recv_sem=vr.at[d],
            device_id=(peer(d), rep), device_id_type=MESH,
        )

    def c_copy(h, d):
        return pltpu.make_async_remote_copy(
            src_ref=csend.at[h, d], dst_ref=crecv.at[h, d],
            send_sem=cs.at[h, d], recv_sem=cr.at[h, d],
            device_id=(peer(d), rep), device_id_type=MESH,
        )

    def pack(d, target, owner):
        for j in range(most):
            target[d, pl.ds(j * rank, rank), :] = vt[tab[0, owner * most + j]]

    def coeffs(d, target, owner):
        extra = csend.shape[2] - depth
        lines = lax.broadcasted_iota(jnp.int32, (extra, part), 0)
        marks = jnp.full((extra, part), clusters, jnp.int32)
        for j in range(most):
            slot = owner * most + j
            value = jnp.dot(ut[tab[0, slot]], field[tab[1, slot]], preferred_element_type=F32)
            kept = lax.broadcasted_iota(jnp.int32, (rank, columns), 0) < tab[2, slot]
            value = jnp.where(kept, value, 0.0).astype(BF16)
            for h in range(PARTS):
                target[h, d, pl.ds(j * rank, rank), :] = value[:, h * part:(h + 1) * part]
            marks = jnp.where(lines == j, tab[3, slot], marks)
        for h in range(PARTS):
            target[h, d, pl.ds(depth, extra), :] = marks.astype(F32).astype(BF16)

    my_rows = pl.ds(pl.multiple_of(rep * share, share), share)

    def halo_copies():
        made = []
        for side, cluster, offset, shift in ((0, clusters - 1, 2, 1), (1, 0, 0, owners - 1)):
            where = (lax.rem(row + shift, owners), rep)
            made.append(pltpu.make_async_remote_copy(
                src_ref=near.at[cluster, offset], dst_ref=hnear.at[side],
                send_sem=hs.at[2 * side], recv_sem=hr.at[2 * side],
                device_id=where, device_id_type=MESH,
            ))
            made.append(pltpu.make_async_remote_copy(
                src_ref=field.at[cluster, my_rows, :], dst_ref=hfield.at[side],
                send_sem=hs.at[2 * side + 1], recv_sem=hr.at[2 * side + 1],
                device_id=where, device_id_type=MESH,
            ))
        return made

    plan = []
    low, size = 0, clusters
    for t in range(stages):
        bit = lax.rem(rep // (1 << t), 2)
        half = size // 2
        partner = rep + (1 << t) * (1 - 2 * bit)
        plan.append((half, partner, low + bit * half, low + (1 - bit) * half))
        low, size = low + bit * half, half

    def labels_of(source, h, d):
        return jnp.concatenate(
            [
                jnp.broadcast_to(source[h, d, pl.ds(depth + j, 1), :].astype(F32), (rank, part))
                for j in range(most)
            ],
            axis=0,
        ).astype(BF16)

    def part_of(right, source, labels, h, d, c):
        label = jnp.asarray(c, jnp.int32).astype(F32).astype(BF16)
        picked = jnp.where(
            labels == label, source[h, d, pl.ds(0, depth), :], jnp.zeros((), BF16)
        )
        return jnp.dot(right[d], picked, preferred_element_type=F32)

    pl.semaphore_wait(barrier, owners + reps - 2)

    @pl.loop(0, peers)
    def _(k):
        d = turn(k)
        pack(d, vsend, peer(d))
        v_copy(d).start()

    halos = halo_copies()
    for copy in halos:
        copy.start()

    @pl.loop(0, peers)
    def _(k):
        d = turn(k)
        coeffs(d, csend, peer(d))
        c_copy(0, d).start()

    for h in range(1, PARTS):
        @pl.loop(0, peers)
        def _(k):
            c_copy(h, turn(k)).start()

    pack(0, vrecv, row)
    coeffs(0, crecv, row)

    def put(c, value):
        for h in range(PARTS):
            total[h, c] = value[:, h * part:(h + 1) * part]

    def add(c, value):
        for h in range(PARTS):
            total[h, c] = total[h, c] + value[:, h * part:(h + 1) * part]

    @pl.loop(0, clusters)
    def _(c):
        put(c, dot_rows(near[c, 1], field[c, my_rows, :]))

    @pl.loop(0, clusters - 1)
    def _(c):
        add(c + 1, dot_rows(near[c, 2], field[c, my_rows, :]))
        add(c, dot_rows(near[c + 1, 0], field[c + 1, my_rows, :]))

    for copy in halos:
        copy.wait_recv()
    add(0, dot_rows(hnear[0], hfield[0]))
    add(clusters - 1, dot_rows(hnear[1], hfield[1]))

    def far(h, d):
        if h == 0:
            vtr[d] = vrecv[d].T
        labels = labels_of(crecv, h, d)

        @pl.loop(0, clusters)
        def _(c):
            total[h, c] = total[h, c] + part_of(vtr, crecv, labels, h, d, c)

    def far_span(h, first, last):
        @pl.loop(first, last)
        def _(k):
            d = turn(peers - 1 - k)
            if h == 0:
                v_copy(d).wait_recv()
            c_copy(h, d).wait_recv()
            far(h, d)

    def r_copy(h, t):
        return pltpu.make_async_remote_copy(
            src_ref=rsend[t].at[h], dst_ref=rrecv[t].at[h],
            send_sem=rs.at[h, t], recv_sem=rr.at[h, t],
            device_id=(row, plan[t][1]), device_id_type=MESH,
        )

    def g_copy(h, t):
        half, partner, keep, _ = plan[t]
        block = out.at[pl.ds(keep, half), :, pl.ds(h * part, part)]
        return pltpu.make_async_remote_copy(
            src_ref=block, dst_ref=block, send_sem=gs.at[h, t], recv_sem=gr.at[h, t],
            device_id=(row, partner), device_id_type=MESH,
        )

    def give(h, t):
        half, _, _, away = plan[t]

        @pl.loop(0, half)
        def _(i):
            rsend[t][h, i] = total[h, away + i].astype(rsend[t].dtype)

        r_copy(h, t).start()

    def take(h, t):
        half, _, keep, _ = plan[t]
        r_copy(h, t).wait_recv()

        @pl.loop(0, half)
        def _(i):
            value = total[h, keep + i] + rrecv[t][h, i].astype(F32)
            if t == stages - 1:
                out[keep + i, :, pl.ds(h * part, part)] = value.astype(BF16)
            else:
                total[h, keep + i] = value

    def sequence(h):
        steps = [lambda: give(h, 0)]
        for t in range(stages):
            if t < stages - 1:
                steps.append(lambda t=t: (take(h, t), give(h, t + 1)))
            else:
                steps.append(lambda t=t: (take(h, t), g_copy(h, t).start()))
        for t in range(stages - 1, 0, -1):
            steps.append(lambda t=t: (g_copy(h, t).wait_recv(), g_copy(h, t - 1).start()))
        steps.append(lambda: g_copy(h, 0).wait_recv())
        return steps

    ahead, behind = sequence(0), sequence(1)
    far(0, 0)
    far_span(0, 0, peers)
    ahead[0]()
    for step in ahead[1:stages]:
        step()
    middle = peers // 2
    far(1, 0)
    far_span(1, 0, middle)
    ahead[stages]()
    far_span(1, middle, peers)
    behind[0]()
    later = ahead[stages + 1:]
    for place, step in enumerate(behind[1:]):
        if place < len(later):
            later[place]()
        step()

    @pl.loop(1, group)
    def _(d):
        v_copy(d).wait_send()
        for h in range(PARTS):
            c_copy(h, d).wait_send()

    for copy in halos:
        copy.wait_send()
    for h in range(PARTS):
        for t in range(stages):
            r_copy(h, t).wait_send()
            g_copy(h, t).wait_send()


def cube(
    most, tab, rowc, ranks, field, ut, vt, near, out,
    cnat, vsend, csend, vcat, ccat, vtr, labels, hnear, hfield, total, acc,
    ksend, krecv, qrecv, gsend, grecv, ysend, yrecv, zsend, zrecv,
    xsend, xrecv, fsend, frecv,
    vs, vr, cs, cr, hs, hr, ks, kr, qs, qr, gs, gr, ys, yr, zs, zr, xs, xr, fs, fr, os, orr,
):
    owners, reps = lax.axis_size("rows"), lax.axis_size("rep")
    row, rep = lax.axis_index("rows"), lax.axis_index("rep")
    half = owners // 2
    w, u, y = row // half, lax.rem(row // 2, 2), lax.rem(row, 2)
    x, core = rep // 2, lax.rem(rep, 2)
    blocks, rank, width = ut.shape
    clusters, _, columns = field.shape
    share = near.shape[2]
    depth = most * rank
    pad = csend.shape[1] - depth
    quad = clusters // 2
    pair = clusters // 4

    def at(w_, u_, y_):
        return w_ * half + u_ * 2 + y_

    def mix(t, one, two):
        return one * (1 - t) + two * t

    to_y = (at(w, u, 1 - y), rep)
    to_z = (at(w, 1 - u, y), rep)
    to_x = (row, (1 - x) * 2 + core)
    to_core = (row, x * 2 + 1 - core)
    to_across = (at(1 - w, u, mix(u, y, x)), mix(u, x, y) * 2 + core)
    after = (lax.rem(row + 1, owners), rep)
    before = (lax.rem(row + owners - 1, owners), rep)
    partners = (to_y, to_z, to_x, to_core, to_across, after, before)

    sends = (
        (to_y, at(1 - w, 0, 1 - y)),
        (to_x, at(1 - w, 1, 1 - x)),
        (to_z, at(w, 1 - u, 1 - y)),
        (to_z, at(w, 1 - u, y)),
    )
    owns = (at(1 - w, 0, y), at(1 - w, 1, x), at(w, u, 1 - y), row)
    bits = (x, y, x, x)
    mine = core * quad
    theirs = (1 - core) * quad

    def remote(src, dst, send, recv, where):
        return pltpu.make_async_remote_copy(
            src_ref=src, dst_ref=dst, send_sem=send, recv_sem=recv,
            device_id=where, device_id_type=MESH,
        )

    def v_copy(i):
        return remote(vsend.at[i], vcat.at[i, pl.ds(depth, depth)], vs.at[i], vr.at[i], sends[i][0])

    def c_copy(i):
        spot = pl.ds(pad + depth, depth + pad)
        return remote(csend.at[i], ccat.at[i, spot], cs.at[i], cr.at[i], sends[i][0])

    def k_copy(i, n):
        return remote(ksend.at[i, n], krecv.at[i, n], ks.at[i, n], kr.at[i, n], to_core)

    def q_copy(n):
        return remote(total.at[theirs + n], qrecv.at[n], qs.at[n], qr.at[n], to_core)

    def g_copy(i, m):
        where = (to_x, to_y)[i]
        return remote(gsend.at[i, m], grecv.at[i, m], gs.at[i, m], gr.at[i, m], where)

    def y_copy(n):
        return remote(ysend.at[n], yrecv.at[n], ys.at[n], yr.at[n], to_y)

    def z_copy(m):
        return remote(zsend.at[m], zrecv.at[m], zs.at[m], zr.at[m], to_z)

    def x_copy(m):
        return remote(xsend.at[m], xrecv.at[m], xs.at[m], xr.at[m], to_across)

    def f_copy(m):
        return remote(fsend.at[m], frecv.at[m], fs.at[m], fr.at[m], to_x)

    def o_copy(m):
        block = out.at[mine + x * pair + m]
        return remote(block, block, os.at[m], orr.at[m], to_x)

    def p_copy(n):
        block = out.at[mine + n]
        return remote(block, block, os.at[pair + n], orr.at[pair + n], to_core)

    barrier = pltpu.get_barrier_semaphore()
    for where in partners:
        pl.semaphore_signal(barrier, inc=1, device_id=where, device_id_type=MESH)

    def pack_v(owner, put):
        for j in range(most):
            put(j * rank, vt[tab[0, owner * most + j]])

    def pack_c(owner, put, put_marks):
        lines = lax.broadcasted_iota(jnp.int32, (pad, columns), 0)
        marks = jnp.full((pad, columns), clusters, jnp.int32)
        for j in range(most):
            slot = owner * most + j
            put(j * rank, cnat[tab[0, slot]])
            marks = jnp.where(lines == j, tab[1, slot], marks)
        put_marks(marks.astype(F32).astype(BF16))

    def send_v(i):
        def put(spot, value):
            vsend[i, pl.ds(spot, rank), :] = value

        pack_v(sends[i][1], put)

    def send_c(i):
        def put(spot, value):
            csend[i, pl.ds(spot, rank), :] = value

        def put_marks(value):
            csend[i, pl.ds(depth, pad), :] = value

        pack_c(sends[i][1], put, put_marks)
        c_copy(i).start()

    def own(i):
        def put_v(spot, value):
            vcat[i, pl.ds(spot, rank), :] = value

        def put_c(spot, value):
            ccat[i, pl.ds(pad + spot, rank), :] = value

        def put_marks(value):
            ccat[i, pl.ds(0, pad), :] = value

        pack_v(owns[i], put_v)
        pack_c(owns[i], put_c, put_marks)

    for i in range(4):
        send_v(i)
    pl.semaphore_wait(barrier, len(partners))
    for i in range(3):
        v_copy(i).start()

    @pl.loop(0, blocks)
    def _(b):
        value = jnp.dot(ut[b], field[rowc[b]], preferred_element_type=F32)
        kept = lax.broadcasted_iota(jnp.int32, (rank, columns), 0) < ranks[b]
        cnat[b] = jnp.where(kept, value, 0.0).astype(BF16)

    for i in range(3):
        send_c(i)
    v_copy(3).start()
    send_c(3)

    my_rows = pl.ds(pl.multiple_of(rep * share, share), share)
    halos = []
    for side, cluster, offset, where in ((0, clusters - 1, 2, after), (1, 0, 0, before)):
        halos.append(remote(
            near.at[cluster, offset], hnear.at[side], hs.at[2 * side], hr.at[2 * side], where
        ))
        halos.append(remote(
            field.at[cluster, my_rows, :], hfield.at[side],
            hs.at[2 * side + 1], hr.at[2 * side + 1], where,
        ))
    for copy in halos:
        copy.start()

    for i in range(4):
        own(i)

    def close(c, offset):
        return dot_rows(near[c, offset], field[c, my_rows, :])

    @pl.loop(1, clusters - 1)
    def _(c):
        total[c] = close(c, 1) + close(c - 1, 2) + close(c + 1, 0)

    last = clusters - 1
    total[0] = close(0, 1) + close(1, 0)
    total[last] = close(last, 1) + close(last - 1, 2)

    def label_rows(i, start, spot):
        for j in range(most):
            line = ccat[i, pl.ds(start + j, 1), :].astype(F32)
            labels[pl.ds(spot + j * rank, rank), :] = (
                jnp.broadcast_to(line, (rank, columns)).astype(BF16)
            )

    def part_of(i, c):
        label = jnp.asarray(c, jnp.int32).astype(F32).astype(BF16)
        picked = jnp.where(
            labels[...] == label, ccat[i, pl.ds(pad, 2 * depth), :], jnp.zeros((), BF16)
        )
        return jnp.dot(vtr[...], picked, preferred_element_type=F32)

    def turn(i, k):
        side = mix(k // pair, 1 - bits[i], bits[i])
        return side * pair + lax.rem(k, pair)

    def partial(i):
        label_rows(i, 0, 0)
        v_copy(i).wait_recv()
        vtr[...] = vcat[i].T
        c_copy(i).wait_recv()
        label_rows(i, pad + 2 * depth, depth)

        @pl.loop(0, quad)
        def _(k):
            n = turn(i, k)
            value = part_of(i, theirs + n)
            if i < 3:
                ksend[i, n] = value.astype(BF16)
                k_copy(i, n).start()
            else:
                total[theirs + n] = total[theirs + n] + value
                q_copy(n).start()

        @pl.loop(0, quad)
        def _(k):
            n = turn(i, k)
            value = part_of(i, mine + n)
            if i < 3:
                acc[i, n] = value
            else:
                total[mine + n] = total[mine + n] + value

    def give_g(i):
        @pl.loop(0, pair)
        def _(m):
            n = (1 - bits[i]) * pair + m
            k_copy(i, n).wait_recv()
            gsend[i, m] = (acc[i, n] + krecv[i, n].astype(F32)).astype(BF16)
            g_copy(i, m).start()

        @pl.loop(0, pair)
        def _(m):
            n = bits[i] * pair + m
            k_copy(i, n).wait_recv()
            acc[i, n] = acc[i, n] + krecv[i, n].astype(F32)

    partial(0)
    partial(1)
    give_g(0)
    partial(2)
    give_g(1)

    @pl.loop(0, quad)
    def _(k):
        n = turn(2, k)
        k_copy(2, n).wait_recv()
        ysend[n] = (acc[2, n] + krecv[2, n].astype(F32)).astype(BF16)
        y_copy(n).start()

    for copy in halos:
        copy.wait_recv()
    total[0] = total[0] + dot_rows(hnear[0], hfield[0])
    total[last] = total[last] + dot_rows(hnear[1], hfield[1])
    partial(3)

    @pl.loop(0, pair)
    def _(m):
        for i in range(2):
            g_copy(i, m).wait_recv()
            n = bits[i] * pair + m
            acc[i, n] = acc[i, n] + grecv[i, m].astype(F32)
        zsend[m] = acc[1 - u, mix(1 - u, x, y) * pair + m].astype(BF16)
        z_copy(m).start()

    @pl.loop(0, pair)
    def _(m):
        z_copy(m).wait_recv()
        value = acc[u, mix(u, x, y) * pair + m] + zrecv[m].astype(F32)
        xsend[m] = value.astype(BF16)
        x_copy(m).start()

    @pl.loop(0, pair)
    def _(m):
        n = (1 - x) * pair + m
        q_copy(n).wait_recv()
        y_copy(n).wait_recv()
        fsend[m] = (total[mine + n] + qrecv[n] + yrecv[n].astype(F32)).astype(BF16)
        f_copy(m).start()

    @pl.loop(0, pair)
    def _(m):
        n = x * pair + m
        q_copy(n).wait_recv()
        y_copy(n).wait_recv()
        value = total[mine + n] + qrecv[n] + yrecv[n].astype(F32)
        f_copy(m).wait_recv()
        value = value + frecv[m].astype(F32)
        x_copy(m).wait_recv()
        out[mine + n] = (value + xrecv[m].astype(F32)).astype(BF16)
        o_copy(m).start()
        p_copy(n).start()

    @pl.loop(0, pair)
    def _(m):
        o_copy(m).wait_recv()
        p_copy((1 - x) * pair + m).start()

    @pl.loop(0, quad)
    def _(n):
        p_copy(n).wait_recv()

    for copy in halos:
        copy.wait_send()
    for i in range(4):
        v_copy(i).wait_send()
        c_copy(i).wait_send()

    @pl.loop(0, quad)
    def _(n):
        for i in range(3):
            k_copy(i, n).wait_send()
        q_copy(n).wait_send()
        y_copy(n).wait_send()
        p_copy(n).wait_send()

    @pl.loop(0, pair)
    def _(m):
        for i in range(2):
            g_copy(i, m).wait_send()
        z_copy(m).wait_send()
        x_copy(m).wait_send()
        f_copy(m).wait_send()
        o_copy(m).wait_send()


def slots_of(col_owner, owners, most):
    target = col_owner[:, 0]
    number = jnp.arange(target.shape[0], dtype=jnp.int32)
    same = (target[:, None] == target[None, :]) & (number[None, :] < number[:, None])
    slot = target * most + jnp.sum(same.astype(jnp.int32), axis=1)
    return slot[:, None] == jnp.arange(owners * most, dtype=jnp.int32)[None, :]


def table(held, clusters, facts):
    lift = [0] * (len(facts) - 1) + [clusters]
    tab = jnp.sum(jnp.where(held[None], jnp.stack(facts)[:, :, None], 0), axis=1)
    return tab + jnp.array(lift, jnp.int32)[:, None]


def shards(
    field_in,
    left_factors,
    right_factors,
    block_ranks,
    row_cluster,
    col_owner,
    col_cluster,
    near_blocks,
):
    owners, reps = lax.axis_size("rows"), lax.axis_size("rep")
    blocks, width, rank = left_factors.shape
    clusters, _, columns = field_in.shape
    share = near_blocks.shape[2]
    most = 5 * blocks // (4 * owners) + 1
    part = columns // PARTS
    depth = most * rank
    pad = -(-most // 16) * 16
    tall = depth + pad
    stages = reps.bit_length() - 1

    held = slots_of(col_owner, owners, most)
    number = jnp.arange(blocks, dtype=jnp.int32)
    smem = pl.BlockSpec(memory_space=pltpu.SMEM)
    vmem = pl.BlockSpec(memory_space=pltpu.VMEM)
    dma = pltpu.SemaphoreType.DMA
    arrays = (
        field_in,
        jnp.swapaxes(left_factors, 1, 2),
        jnp.swapaxes(right_factors, 1, 2),
        near_blocks,
    )
    cubic = stages == 2 and owners == 2 ** 3
    if cubic:
        quad, pair = clusters // 2, clusters // 4
        slab = (width, columns)
        gathered = pl.pallas_call(
            functools.partial(cube, most),
            out_shape=jax.ShapeDtypeStruct(field_in.shape, BF16),
            in_specs=[smem] * 3 + [vmem] * 4,
            out_specs=vmem,
            scratch_shapes=[
                pltpu.VMEM((blocks, rank, columns), BF16),
                pltpu.VMEM((4, depth, width), BF16),
                pltpu.VMEM((4, tall, columns), BF16),
                pltpu.VMEM((4, 2 * depth, width), BF16),
                pltpu.VMEM((4, 2 * tall, columns), BF16),
                pltpu.VMEM((width, 2 * depth), BF16),
                pltpu.VMEM((2 * depth, columns), BF16),
                pltpu.VMEM((2, share, width), BF16),
                pltpu.VMEM((2, share, columns), BF16),
                pltpu.VMEM((clusters, *slab), F32),
                pltpu.VMEM((3, quad, *slab), F32),
                pltpu.VMEM((3, quad, *slab), BF16),
                pltpu.VMEM((3, quad, *slab), BF16),
                pltpu.VMEM((quad, *slab), F32),
                pltpu.VMEM((2, pair, *slab), BF16),
                pltpu.VMEM((2, pair, *slab), BF16),
                pltpu.VMEM((quad, *slab), BF16),
                pltpu.VMEM((quad, *slab), BF16),
                *[pltpu.VMEM((pair, *slab), BF16)] * 6,
                *[dma((4,))] * 6,
                *[dma((3, quad))] * 2,
                *[dma((quad,))] * 2,
                *[dma((2, pair))] * 2,
                *[dma((quad,))] * 2,
                *[dma((pair,))] * 6,
                *[dma((pair + quad,))] * 2,
            ],
            compiler_params=pltpu.CompilerParams(
                collective_id=0, has_side_effects=True, vmem_limit_bytes=60 * 1024 * 1024
            ),
        )(table(held, clusters, [number, col_cluster - clusters]), row_cluster, block_ranks, *arrays)
        return gathered.astype(F32)

    halves = [clusters >> (t + 1) for t in range(stages)]
    steps = [
        pltpu.VMEM((PARTS, half, width, part), BF16 if t else F32) for t, half in enumerate(halves)
    ]
    gathered = pl.pallas_call(
        functools.partial(kernel, owners, reps, most),
        out_shape=jax.ShapeDtypeStruct(field_in.shape, BF16),
        in_specs=[smem] + [vmem] * 4,
        out_specs=vmem,
        scratch_shapes=[
            pltpu.VMEM((owners, depth, width), BF16),
            pltpu.VMEM((owners, depth, width), BF16),
            pltpu.VMEM((owners, width, depth), BF16),
            pltpu.VMEM((PARTS, owners, tall, part), BF16),
            pltpu.VMEM((PARTS, owners, tall, part), BF16),
            pltpu.VMEM((2, share, width), BF16),
            pltpu.VMEM((2, share, columns), BF16),
            pltpu.VMEM((PARTS, clusters, width, part), F32),
            *steps,
            *steps,
            dma((owners,)),
            dma((owners,)),
            dma((PARTS, owners)),
            dma((PARTS, owners)),
            dma((4,)),
            dma((4,)),
            *[dma((PARTS, stages))] * 4,
        ],
        compiler_params=pltpu.CompilerParams(
            collective_id=0, has_side_effects=True, vmem_limit_bytes=60 * 1024 * 1024
        ),
    )(table(held, clusters, [number, row_cluster, block_ranks, col_cluster - clusters]), *arrays)
    return gathered.astype(F32)


def solution(mesh):
    in_specs = (
        P("rows", None, None),
        P(("rows", "rep"), None, None),
        P(("rows", "rep"), None, None),
        P(("rows", "rep")),
        P(("rows", "rep")),
        P(("rows", "rep"), None),
        P(("rows", "rep")),
        P("rows", None, "rep", None),
    )
    out_specs = P("rows", None, None)
    return jax.shard_map(shards, mesh=mesh, in_specs=in_specs, out_specs=out_specs, check_vma=False)
```

time: 121 us -> 82.1 us (0.68)
  the two profiles are of different devices: /device:TPU:0 before, /device:TPU:9 now
where the time goes in v1:
time: 82.1 us; the launch traced here: 82 us
  Pallas kernels  75.5 us (92%)
  other arithmetic  6.4 us (8%)
    pallas_call x1, Pallas kernels, shards(): pl.pallas_call(functools.partial(cube, most), out_shape=jax.ShapeDtypeStr...  75.5 us
    convert_element_type x1, other arithmetic, shards(): return gathered.astype(F32)  3.36 us

profile of v1, /device:TPU:9, one launch (start us, length us, event | category | flops | bytes accessed | tf_op | source)
XLA Modules:
  0.0 82.0 jit_solution(12602350947432888525)
XLA Ops:
  0.0 0.7 add_bitcast_fusion
  0.7 0.9 %convert_reduce_fusion = s32[32]{0:T(128)S(1)} fusion(s32[32]{0:T(128)} %bitcast.13), kind=kLoop, calls=%fused_computation.2 | loop fusion | flops 5088 | bytes 256 | tf_op jit(solution)/shard_map/reduce_sum | solution.py:611
  1.6 0.7 fusion.1
  2.3 0.1 iota_compare_fusion
  2.3 0.1 select_reduce_fusion
  2.4 0.6 broadcast_add_fusion.tab
  3.1 75.5 %shard_map.91 = bf16[8,384,256]{2,1,0:T(8,128)(2,1)} custom-call(s32[2,48]{1,0:T(2,128)} %broadcast_add_fusion.tab, s32[32]{0:T(128)} %rowc.1, s32[32]{0:T(128)} %ranks.1, bf16[8,384,256]{2,1,0:T(8,128)(2,1)} %field.1, bf16[32,64,384]{2,1,0:T(8,128)(2,1)} %bitcast.11, bf16[32,64,384]{2,1,0:T(8,128)(2,1)} %bitcast.12, bf16[8,3,96,384]{3,2,1,0:T(8,128)(2,1)} %near.1), custom_call_target="tpu_custom_call" | custom-call | tf_op jit(solution)/shard_map/pallas_call | solution.py:657
  78.6 3.4 %convert_element_type.7 = f32[8,384,256]{2,1,0:T(8,128)} convert(bf16[8,384,256]{2,1,0:T(8,128)(2,1)} %shard_map.91) | non-fusion elementwise | flops 786432 | bytes 4718592 | tf_op jit(solution)/shard_map/convert_element_type | solution.py:694
  (3 shorter events, 0.0 us)

commit v2 on v1

--- a/solution.py
+++ b/solution.py
@@ -9,6 +9,7 @@
 
 MESH = pl.DeviceIdType.MESH
 PARTS = 2
+SPLIT = 2
 BF16 = jnp.bfloat16
 F32 = jnp.float32
 
@@ -278,11 +279,12 @@
 
 
 def cube(
-    most, tab, rowc, ranks, field, ut, vt, near, out,
-    cnat, vsend, csend, vcat, ccat, vtr, labels, hnear, hfield, total, acc,
+    most, rowc, ranks, tab, field_hbm, ut_hbm, vt_hbm, near_hbm, out,
+    field, ut, vt, near,
+    cnat, vsend, csend, vrecv, crecv, vown, cown, vtr, labels, hnear, hfield, total, acc,
     ksend, krecv, qrecv, gsend, grecv, ysend, yrecv, zsend, zrecv,
     xsend, xrecv, fsend, frecv,
-    vs, vr, cs, cr, hs, hr, ks, kr, qs, qr, gs, gr, ys, yr, zs, zr, xs, xr, fs, fr, os, orr,
+    ins, vs, vr, cs, cr, hs, hr, ks, kr, qs, qr, gs, gr, ys, yr, zs, zr, xs, xr, fs, fr, os, orr,
 ):
     owners, reps = lax.axis_size("rows"), lax.axis_size("rep")
     row, rep = lax.axis_index("rows"), lax.axis_index("rep")
@@ -293,9 +295,11 @@
     clusters, _, columns = field.shape
     share = near.shape[2]
     depth = most * rank
-    pad = csend.shape[1] - depth
+    pad = vsend.shape[1] - depth
     quad = clusters // 2
     pair = clusters // 4
+    sub = width // SPLIT
+    bits_of = (blocks - 1).bit_length()
 
     def at(w_, u_, y_):
         return w_ * half + u_ * 2 + y_
@@ -308,9 +312,22 @@
     to_x = (row, (1 - x) * 2 + core)
     to_core = (row, x * 2 + 1 - core)
     to_across = (at(1 - w, u, mix(u, y, x)), mix(u, x, y) * 2 + core)
-    after = (lax.rem(row + 1, owners), rep)
-    before = (lax.rem(row + owners - 1, owners), rep)
-    partners = (to_y, to_z, to_x, to_core, to_across, after, before)
+    to_next = (lax.rem(row + mix(y, owners - 2, 2), owners), rep)
+    to_prior = (lax.rem(row + mix(y, 2, owners - 2), owners), rep)
+    partners = (to_y, to_z, to_x, to_core, to_across, to_next, to_prior)
+
+    barrier = pltpu.get_barrier_semaphore()
+    for where in partners:
+        pl.semaphore_signal(barrier, inc=1, device_id=where, device_id_type=MESH)
+
+    loads = [
+        pltpu.make_async_copy(src, dst, ins.at[i])
+        for i, (src, dst) in enumerate(
+            ((vt_hbm, vt), (ut_hbm, ut), (field_hbm, field), (near_hbm, near))
+        )
+    ]
+    for load in loads:
+        load.start()
 
     sends = (
         (to_y, at(1 - w, 0, 1 - y)),
@@ -330,11 +347,10 @@
         )
 
     def v_copy(i):
-        return remote(vsend.at[i], vcat.at[i, pl.ds(depth, depth)], vs.at[i], vr.at[i], sends[i][0])
+        return remote(vsend.at[i], vrecv.at[i], vs.at[i], vr.at[i], sends[i][0])
 
     def c_copy(i):
-        spot = pl.ds(pad + depth, depth + pad)
-        return remote(csend.at[i], ccat.at[i, spot], cs.at[i], cr.at[i], sends[i][0])
+        return remote(csend.at[i], crecv.at[i], cs.at[i], cr.at[i], sends[i][0])
 
     def k_copy(i, n):
         return remote(ksend.at[i, n], krecv.at[i, n], ks.at[i, n], kr.at[i, n], to_core)
@@ -359,226 +375,286 @@
         return remote(fsend.at[m], frecv.at[m], fs.at[m], fr.at[m], to_x)
 
     def o_copy(m):
-        block = out.at[mine + x * pair + m]
+        block = out.at[(mine + x * pair) * SPLIT + m]
         return remote(block, block, os.at[m], orr.at[m], to_x)
 
     def p_copy(n):
-        block = out.at[mine + n]
-        return remote(block, block, os.at[pair + n], orr.at[pair + n], to_core)
-
-    barrier = pltpu.get_barrier_semaphore()
-    for where in partners:
-        pl.semaphore_signal(barrier, inc=1, device_id=where, device_id_type=MESH)
+        block = out.at[mine * SPLIT + n]
+        spot = pair * SPLIT + n
+        return remote(block, block, os.at[spot], orr.at[spot], to_core)
 
     def pack_v(owner, put):
+        lines = lax.broadcasted_iota(jnp.int32, (pad, width), 0)
+        marks = jnp.full((pad, width), clusters, jnp.int32)
         for j in range(most):
-            put(j * rank, vt[tab[0, owner * most + j]])
-
-    def pack_c(owner, put, put_marks):
-        lines = lax.broadcasted_iota(jnp.int32, (pad, columns), 0)
-        marks = jnp.full((pad, columns), clusters, jnp.int32)
+            put(pl.ds(j * rank, rank), vt[tab[0, owner * most + j]])
+            label = tab[1, owner * most + j]
+            marks = jnp.where(lines == j, label, marks)
+        put(pl.ds(depth, pad), marks.astype(F32).astype(BF16))
+
+    def pack_c(owner, put):
         for j in range(most):
-            slot = owner * most + j
-            put(j * rank, cnat[tab[0, slot]])
-            marks = jnp.where(lines == j, tab[1, slot], marks)
-        put_marks(marks.astype(F32).astype(BF16))
+            put(pl.ds(j * rank, rank), cnat[tab[0, owner * most + j]])
 
     def send_v(i):
         def put(spot, value):
-            vsend[i, pl.ds(spot, rank), :] = value
+            vsend[i, spot, :] = value
 
         pack_v(sends[i][1], put)
 
     def send_c(i):
         def put(spot, value):
-            csend[i, pl.ds(spot, rank), :] = value
-
-        def put_marks(value):
-            csend[i, pl.ds(depth, pad), :] = value
-
-        pack_c(sends[i][1], put, put_marks)
+            csend[i, spot, :] = value
+
+        pack_c(sends[i][1], put)
         c_copy(i).start()
 
-    def own(i):
-        def put_v(spot, value):
-            vcat[i, pl.ds(spot, rank), :] = value
-
-        def put_c(spot, value):
-            ccat[i, pl.ds(pad + spot, rank), :] = value
-
-        def put_marks(value):
-            ccat[i, pl.ds(0, pad), :] = value
-
-        pack_v(owns[i], put_v)
-        pack_c(owns[i], put_c, put_marks)
-
+    my_rows = pl.ds(pl.multiple_of(rep * share, share), share)
+    last = clusters - 1
+    halos = [
+        remote(near.at[y * last, y * 2], hnear, hs.at[0], hr.at[0], to_next),
+        remote(field.at[y * last, my_rows, :], hfield, hs.at[1], hr.at[1], to_next),
+    ]
+
+    loads[0].wait()
     for i in range(4):
         send_v(i)
+    for load in loads[1:]:
+        load.wait()
     pl.semaphore_wait(barrier, len(partners))
-    for i in range(3):
+    for i in range(2):
         v_copy(i).start()
-
-    @pl.loop(0, blocks)
-    def _(b):
+    for copy in halos:
+        copy.start()
+    v_copy(2).start()
+
+    def coefficients(b):
         value = jnp.dot(ut[b], field[rowc[b]], preferred_element_type=F32)
         kept = lax.broadcasted_iota(jnp.int32, (rank, columns), 0) < ranks[b]
         cnat[b] = jnp.where(kept, value, 0.0).astype(BF16)
+
+    @pl.loop(0, blocks // 4)
+    def _(b):
+        for e in range(4):
+            coefficients(b * 4 + e)
 
     for i in range(3):
         send_c(i)
     v_copy(3).start()
     send_c(3)
 
-    my_rows = pl.ds(pl.multiple_of(rep * share, share), share)
-    halos = []
-    for side, cluster, offset, where in ((0, clusters - 1, 2, after), (1, 0, 0, before)):
-        halos.append(remote(
-            near.at[cluster, offset], hnear.at[side], hs.at[2 * side], hr.at[2 * side], where
-        ))
-        halos.append(remote(
-            field.at[cluster, my_rows, :], hfield.at[side],
-            hs.at[2 * side + 1], hr.at[2 * side + 1], where,
-        ))
-    for copy in halos:
-        copy.start()
-
-    for i in range(4):
-        own(i)
+    def cut(value):
+        return [value[s * sub:(s + 1) * sub] for s in range(SPLIT)]
+
+    def prepare(d, factors):
+        vtr[d] = factors[pl.ds(0, depth), :].T
+        for j in range(most):
+            line = factors[pl.ds(depth + j, 1), pl.ds(0, columns)].astype(F32)
+            labels[d, pl.ds(j * rank, rank), :] = (
+                jnp.broadcast_to(line, (rank, columns)).astype(BF16)
+            )
+
+    def part_of(d, coeffs, c):
+        label = jnp.asarray(c, jnp.int32).astype(F32).astype(BF16)
+        picked = jnp.where(labels[d] == label, coeffs[...], jnp.zeros((), BF16))
+        return jnp.dot(vtr[d], picked, preferred_element_type=F32)
+
+    def own(i):
+        def put_v(spot, value):
+            vown[spot, :] = value
+
+        def put_c(spot, value):
+            cown[spot, :] = value
+
+        pack_v(owns[i], put_v)
+        pack_c(owns[i], put_c)
+        prepare(3, vown)
+
+        @pl.loop(0, clusters // 2)
+        def _(k):
+            for e in range(2):
+                c = 2 * k + e
+                for s, value in enumerate(cut(part_of(3, cown, c))):
+                    if i < 3:
+                        acc[i, c * SPLIT + s] = value
+                    else:
+                        total[c, s] = value
 
     def close(c, offset):
         return dot_rows(near[c, offset], field[c, my_rows, :])
 
-    @pl.loop(1, clusters - 1)
-    def _(c):
-        total[c] = close(c, 1) + close(c - 1, 2) + close(c + 1, 0)
-
-    last = clusters - 1
-    total[0] = close(0, 1) + close(1, 0)
-    total[last] = close(last, 1) + close(last - 1, 2)
-
-    def label_rows(i, start, spot):
-        for j in range(most):
-            line = ccat[i, pl.ds(start + j, 1), :].astype(F32)
-            labels[pl.ds(spot + j * rank, rank), :] = (
-                jnp.broadcast_to(line, (rank, columns)).astype(BF16)
-            )
-
-    def part_of(i, c):
-        label = jnp.asarray(c, jnp.int32).astype(F32).astype(BF16)
-        picked = jnp.where(
-            labels[...] == label, ccat[i, pl.ds(pad, 2 * depth), :], jnp.zeros((), BF16)
-        )
-        return jnp.dot(vtr[...], picked, preferred_element_type=F32)
+    def raise_total(c, value):
+        for s, piece in enumerate(cut(value)):
+            total[c, s] = total[c, s] + piece
+
+    def raise_acc(c, value):
+        for s, piece in enumerate(cut(value)):
+            acc[2, c * SPLIT + s] = acc[2, c * SPLIT + s] + piece
+
+    def near_field():
+        @pl.loop(1, last)
+        def _(c):
+            raise_total(c, close(c, 1) + close(c - 1, 2) + close(c + 1, 0))
+
+        raise_total(0, close(0, 1) + close(1, 0))
+        raise_total(last, close(last, 1) + close(last - 1, 2))
+
+    def halo_terms():
+        for copy in halos:
+            copy.wait_recv()
+        raise_acc(y * last, close((1 - y) * last, (1 - y) * 2))
+        raise_acc((1 - y) * last, dot_rows(hnear[...], hfield[...]))
 
     def turn(i, k):
         side = mix(k // pair, 1 - bits[i], bits[i])
         return side * pair + lax.rem(k, pair)
 
-    def partial(i):
-        label_rows(i, 0, 0)
+    def ready(i):
         v_copy(i).wait_recv()
-        vtr[...] = vcat[i].T
+        prepare(min(i, 2), vrecv.at[i])
+
+    def partial_away(i):
         c_copy(i).wait_recv()
-        label_rows(i, pad + 2 * depth, depth)
-
-        @pl.loop(0, quad)
+
+        @pl.loop(0, quad // 2)
         def _(k):
-            n = turn(i, k)
-            value = part_of(i, theirs + n)
-            if i < 3:
-                ksend[i, n] = value.astype(BF16)
-                k_copy(i, n).start()
-            else:
-                total[theirs + n] = total[theirs + n] + value
-                q_copy(n).start()
-
-        @pl.loop(0, quad)
+            for e in range(2):
+                n = turn(i, 2 * k + e)
+                c = theirs + n
+                value = part_of(min(i, 2), crecv.at[i], c)
+                if i < 3:
+                    for s, piece in enumerate(cut(value)):
+                        ksend[i, n, s] = (acc[i, c * SPLIT + s] + piece).astype(BF16)
+                    k_copy(i, n).start()
+                else:
+                    raise_total(c, value)
+                    q_copy(n).start()
+
+    def partial_keep(i, first, count):
+        @pl.loop(0, count // 2)
         def _(k):
-            n = turn(i, k)
-            value = part_of(i, mine + n)
-            if i < 3:
-                acc[i, n] = value
-            else:
-                total[mine + n] = total[mine + n] + value
+            for e in range(2):
+                c = mine + turn(i, first + 2 * k + e)
+                value = part_of(min(i, 2), crecv.at[i], c)
+                if i < 3:
+                    for s, piece in enumerate(cut(value)):
+                        acc[i, c * SPLIT + s] = acc[i, c * SPLIT + s] + piece
+                else:
+                    raise_total(c, value)
+
+    def summed(i, n, s):
+        return acc[i, (mine + n) * SPLIT + s] + krecv[i, n, s].astype(F32)
 
     def give_g(i):
+        partial_keep(i, 0, pair)
+
         @pl.loop(0, pair)
         def _(m):
             n = (1 - bits[i]) * pair + m
             k_copy(i, n).wait_recv()
-            gsend[i, m] = (acc[i, n] + krecv[i, n].astype(F32)).astype(BF16)
-            g_copy(i, m).start()
-
+            for s in range(SPLIT):
+                gsend[i, m * SPLIT + s] = summed(i, n, s).astype(BF16)
+                g_copy(i, m * SPLIT + s).start()
+
+    def give_y():
+        @pl.loop(0, quad)
+        def _(k):
+            n = turn(2, k)
+            k_copy(2, n).wait_recv()
+            for s in range(SPLIT):
+                ysend[n, s] = summed(2, n, s).astype(BF16)
+            y_copy(n).start()
+
+    def take_k(i):
         @pl.loop(0, pair)
         def _(m):
-            n = bits[i] * pair + m
-            k_copy(i, n).wait_recv()
-            acc[i, n] = acc[i, n] + krecv[i, n].astype(F32)
-
-    partial(0)
-    partial(1)
-    give_g(0)
-    partial(2)
-    give_g(1)
-
-    @pl.loop(0, quad)
-    def _(k):
-        n = turn(2, k)
-        k_copy(2, n).wait_recv()
-        ysend[n] = (acc[2, n] + krecv[2, n].astype(F32)).astype(BF16)
-        y_copy(n).start()
-
-    for copy in halos:
-        copy.wait_recv()
-    total[0] = total[0] + dot_rows(hnear[0], hfield[0])
-    total[last] = total[last] + dot_rows(hnear[1], hfield[1])
-    partial(3)
-
-    @pl.loop(0, pair)
-    def _(m):
-        for i in range(2):
-            g_copy(i, m).wait_recv()
-            n = bits[i] * pair + m
-            acc[i, n] = acc[i, n] + grecv[i, m].astype(F32)
-        zsend[m] = acc[1 - u, mix(1 - u, x, y) * pair + m].astype(BF16)
-        z_copy(m).start()
-
-    @pl.loop(0, pair)
-    def _(m):
-        z_copy(m).wait_recv()
-        value = acc[u, mix(u, x, y) * pair + m] + zrecv[m].astype(F32)
-        xsend[m] = value.astype(BF16)
-        x_copy(m).start()
-
-    @pl.loop(0, pair)
-    def _(m):
+            k_copy(i, bits[i] * pair + m).wait_recv()
+
+    def reduced(t, m, s):
+        return acc[t, (mine + mix(t, x, y) * pair + m) * SPLIT + s]
+
+    def pass_z(m):
+        for s in range(SPLIT):
+            for i in range(2):
+                g_copy(i, m * SPLIT + s).wait_recv()
+                n = bits[i] * pair + m
+                value = summed(i, n, s) + grecv[i, m * SPLIT + s].astype(F32)
+                acc[i, (mine + n) * SPLIT + s] = value
+            zsend[m * SPLIT + s] = reduced(1 - u, m, s).astype(BF16)
+            z_copy(m * SPLIT + s).start()
+
+    def pass_x(m):
+        for s in range(SPLIT):
+            z_copy(m * SPLIT + s).wait_recv()
+            value = reduced(u, m, s) + zrecv[m * SPLIT + s].astype(F32)
+            xsend[m * SPLIT + s] = value.astype(BF16)
+            x_copy(m * SPLIT + s).start()
+
+    def gathered(n, s):
+        return total[mine + n, s] + qrecv[n, s] + yrecv[n, s].astype(F32)
+
+    def pass_f(m):
         n = (1 - x) * pair + m
         q_copy(n).wait_recv()
         y_copy(n).wait_recv()
-        fsend[m] = (total[mine + n] + qrecv[n] + yrecv[n].astype(F32)).astype(BF16)
-        f_copy(m).start()
+        for s in range(SPLIT):
+            fsend[m * SPLIT + s] = gathered(n, s).astype(BF16)
+            f_copy(m * SPLIT + s).start()
+
+    for i in (1, 0, 2):
+        own(i)
+    ready(1)
+    ready(0)
+    own(3)
+    ready(2)
+    partial_away(1)
+    partial_away(0)
+    give_g(1)
+    give_g(0)
+    halo_terms()
+    partial_away(2)
+    partial_keep(2, 0, quad)
+    give_y()
+    partial_keep(1, pair, pair)
+    partial_keep(0, pair, pair)
+    take_k(1)
+    take_k(0)
+    near_field()
+    pass_z(0)
+    ready(3)
+    partial_away(3)
+    for m in range(1, pair):
+        pass_z(m)
+    partial_keep(3, 0, quad)
+
+    @pl.loop(0, pair)
+    def _(m):
+        pass_x(m)
+        pass_f(m)
 
     @pl.loop(0, pair)
     def _(m):
         n = x * pair + m
         q_copy(n).wait_recv()
         y_copy(n).wait_recv()
-        value = total[mine + n] + qrecv[n] + yrecv[n].astype(F32)
-        f_copy(m).wait_recv()
-        value = value + frecv[m].astype(F32)
-        x_copy(m).wait_recv()
-        out[mine + n] = (value + xrecv[m].astype(F32)).astype(BF16)
-        o_copy(m).start()
-        p_copy(n).start()
-
-    @pl.loop(0, pair)
+        for s in range(SPLIT):
+            piece = m * SPLIT + s
+            f_copy(piece).wait_recv()
+            value = gathered(n, s) + frecv[piece].astype(F32)
+            x_copy(piece).wait_recv()
+            out[(mine + n) * SPLIT + s] = (value + xrecv[piece].astype(F32)).astype(BF16)
+            o_copy(piece).start()
+            p_copy(n * SPLIT + s).start()
+
+    @pl.loop(0, pair * SPLIT)
     def _(m):
         o_copy(m).wait_recv()
-        p_copy((1 - x) * pair + m).start()
-
-    @pl.loop(0, quad)
+        p_copy((1 - x) * pair * SPLIT + m).start()
+
+    @pl.loop(0, quad * SPLIT)
     def _(n):
         p_copy(n).wait_recv()
+        p_copy(n).wait_send()
 
     for copy in halos:
         copy.wait_send()
@@ -592,9 +668,8 @@
             k_copy(i, n).wait_send()
         q_copy(n).wait_send()
         y_copy(n).wait_send()
-        p_copy(n).wait_send()
-
-    @pl.loop(0, pair)
+
+    @pl.loop(0, pair * SPLIT)
     def _(m):
         for i in range(2):
             g_copy(i, m).wait_send()
@@ -639,8 +714,6 @@
     tall = depth + pad
     stages = reps.bit_length() - 1
 
-    held = slots_of(col_owner, owners, most)
-    number = jnp.arange(blocks, dtype=jnp.int32)
     smem = pl.BlockSpec(memory_space=pltpu.SMEM)
     vmem = pl.BlockSpec(memory_space=pltpu.VMEM)
     dma = pltpu.SemaphoreType.DMA
@@ -650,49 +723,56 @@
         jnp.swapaxes(right_factors, 1, 2),
         near_blocks,
     )
-    cubic = stages == 2 and owners == 2 ** 3
+    cubic = stages == 2 and owners == 2 ** 3 and (blocks - 1).bit_length() * most < 32
+    cubic = cubic and columns <= width
     if cubic:
         quad, pair = clusters // 2, clusters // 4
-        slab = (width, columns)
+        slab = (width // SPLIT, columns)
+        keep = pltpu.VMEM
         gathered = pl.pallas_call(
             functools.partial(cube, most),
-            out_shape=jax.ShapeDtypeStruct(field_in.shape, BF16),
-            in_specs=[smem] * 3 + [vmem] * 4,
+            out_shape=jax.ShapeDtypeStruct((clusters * SPLIT, *slab), BF16),
+            in_specs=[smem] * 3 + [pl.BlockSpec(memory_space=pl.ANY)] * 4,
             out_specs=vmem,
             scratch_shapes=[
-                pltpu.VMEM((blocks, rank, columns), BF16),
-                pltpu.VMEM((4, depth, width), BF16),
-                pltpu.VMEM((4, tall, columns), BF16),
-                pltpu.VMEM((4, 2 * depth, width), BF16),
-                pltpu.VMEM((4, 2 * tall, columns), BF16),
-                pltpu.VMEM((width, 2 * depth), BF16),
-                pltpu.VMEM((2 * depth, columns), BF16),
-                pltpu.VMEM((2, share, width), BF16),
-                pltpu.VMEM((2, share, columns), BF16),
-                pltpu.VMEM((clusters, *slab), F32),
-                pltpu.VMEM((3, quad, *slab), F32),
-                pltpu.VMEM((3, quad, *slab), BF16),
-                pltpu.VMEM((3, quad, *slab), BF16),
-                pltpu.VMEM((quad, *slab), F32),
-                pltpu.VMEM((2, pair, *slab), BF16),
-                pltpu.VMEM((2, pair, *slab), BF16),
-                pltpu.VMEM((quad, *slab), BF16),
-                pltpu.VMEM((quad, *slab), BF16),
-                *[pltpu.VMEM((pair, *slab), BF16)] * 6,
-                *[dma((4,))] * 6,
+                *[keep(array.shape, BF16) for array in arrays],
+                keep((blocks, rank, columns), BF16),
+                keep((4, tall, width), BF16),
+                keep((4, depth, columns), BF16),
+                keep((4, tall, width), BF16),
+                keep((4, depth, columns), BF16),
+                keep((tall, width), BF16),
+                keep((depth, columns), BF16),
+                keep((4, width, depth), BF16),
+                keep((4, depth, columns), BF16),
+                keep((share, width), BF16),
+                keep((share, columns), BF16),
+                keep((clusters, SPLIT, *slab), F32),
+                keep((3, clusters * SPLIT, *slab), F32),
+                keep((3, quad, SPLIT, *slab), BF16),
+                keep((3, quad, SPLIT, *slab), BF16),
+                keep((quad, SPLIT, *slab), F32),
+                keep((2, pair * SPLIT, *slab), BF16),
+                keep((2, pair * SPLIT, *slab), BF16),
+                keep((quad, SPLIT, *slab), BF16),
+                keep((quad, SPLIT, *slab), BF16),
+                *[keep((pair * SPLIT, *slab), BF16)] * 6,
+                *[dma((4,))] * 7,
                 *[dma((3, quad))] * 2,
                 *[dma((quad,))] * 2,
-                *[dma((2, pair))] * 2,
+                *[dma((2, pair * SPLIT))] * 2,
                 *[dma((quad,))] * 2,
-                *[dma((pair,))] * 6,
-                *[dma((pair + quad,))] * 2,
+                *[dma((pair * SPLIT,))] * 6,
+                *[dma(((pair + quad) * SPLIT,))] * 2,
             ],
             compiler_params=pltpu.CompilerParams(
                 collective_id=0, has_side_effects=True, vmem_limit_bytes=60 * 1024 * 1024
             ),
-        )(table(held, clusters, [number, col_cluster - clusters]), row_cluster, block_ranks, *arrays)
-        return gathered.astype(F32)
-
+        )(row_cluster, block_ranks, table(slots_of(col_owner, owners, most), clusters, [jnp.arange(blocks, dtype=jnp.int32), col_cluster - clusters]), *arrays)
+        return gathered.reshape(field_in.shape).astype(F32)
+
+    held = slots_of(col_owner, owners, most)
+    number = jnp.arange(blocks, dtype=jnp.int32)
     halves = [clusters >> (t + 1) for t in range(stages)]
     steps = [
         pltpu.VMEM((PARTS, half, width, part), BF16 if t else F32) for t, half in enumerate(halves)

time: 82.1 us -> 71.7 us (0.87)
  Pallas kernels: 75.5 us -> 65.1 us
    pallas_call x1, Pallas kernels: 75.5 us -> 65.1 us  [shards(): pl.pallas_call(functools.partial(cube, most), out_shape=jax.ShapeDtypeStr...]
where the time goes in v2:
time: 71.7 us; the launch traced here: 71.5 us
  Pallas kernels  65.1 us (91%)
  other arithmetic  6.4 us (9%)
    pallas_call x1, Pallas kernels, shards(): pl.pallas_call(functools.partial(cube, most), out_shape=jax.ShapeDtypeStr...  65.1 us
    convert_element_type x1, other arithmetic, shards(): return gathered.reshape(field_in.shape).astype(F32)  3.36 us

profile of v2, /device:TPU:9, one launch (start us, length us, event | category | flops | bytes accessed | tf_op | source)
XLA Modules:
  0.0 71.5 jit_solution(15252653129270809352)
XLA Ops:
  0.0 0.7 add_bitcast_fusion
  0.7 0.9 %convert_reduce_fusion = s32[32]{0:T(128)S(1)} fusion(s32[32]{0:T(128)} %bitcast.18), kind=kLoop, calls=%fused_computation.3 | loop fusion | flops 5088 | bytes 256 | tf_op jit(solution)/shard_map/reduce_sum | solution.py:686
  1.6 0.7 fusion.1
  2.3 0.1 iota_compare_fusion
  2.3 0.1 select_reduce_fusion
  2.4 0.6 broadcast_add_fusion.tab
  3.1 65.1 %shard_map.91 = bf16[16,192,256]{2,1,0:T(8,128)(2,1)} custom-call(s32[32]{0:T(128)} %rowc.1, s32[32]{0:T(128)} %ranks.1, s32[2,48]{1,0:T(2,128)} %broadcast_add_fusion.tab, bf16[8,384,256]{2,1,0:T(8,128)(2,1)} %field_hbm.1, bf16[32,64,384]{2,1,0:T(8,128)(2,1)} %bitcast.16, bf16[32,64,384]{2,1,0:T(8,128)(2,1)} %bitcast.17, bf16[8,3,96,384]{3,2,1,0:T(8,128)(2,1)} %near_hbm.1), custom_call_target="tpu_custom_call" | custom-call | tf_op jit(solution)/shard_map/pallas_call | solution.py:732
  68.2 3.4 %bitcast_convert_fusion = f32[8,384,256]{2,1,0:T(8,128)} fusion(bf16[8,384,256]{2,1,0:T(8,128)(2,1)} %bitcast.15), kind=kLoop, calls=%fused_computation | loop fusion | flops 786432 | bytes 4718592 | tf_op jit(solution)/shard_map/convert_element_type | solution.py:772
  (3 shorter events, 0.0 us)

commit v3 on v2

--- a/solution.py
+++ b/solution.py
@@ -10,6 +10,7 @@
 MESH = pl.DeviceIdType.MESH
 PARTS = 2
 SPLIT = 2
+SPOTS = (0, 0, 1, 1)
 BF16 = jnp.bfloat16
 F32 = jnp.float32
 
@@ -279,7 +280,7 @@
 
 
 def cube(
-    most, rowc, ranks, tab, field_hbm, ut_hbm, vt_hbm, near_hbm, out,
+    most, rowc, ranks, owner_of, colc, field_hbm, ut_hbm, vt_hbm, near_hbm, out,
     field, ut, vt, near,
     cnat, vsend, csend, vrecv, crecv, vown, cown, vtr, labels, hnear, hfield, total, acc,
     ksend, krecv, qrecv, gsend, grecv, ysend, yrecv, zsend, zrecv,
@@ -311,7 +312,7 @@
     to_z = (at(w, 1 - u, y), rep)
     to_x = (row, (1 - x) * 2 + core)
     to_core = (row, x * 2 + 1 - core)
-    to_across = (at(1 - w, u, mix(u, y, x)), mix(u, x, y) * 2 + core)
+    to_across = (at(1 - w, u, y), rep)
     to_next = (lax.rem(row + mix(y, owners - 2, 2), owners), rep)
     to_prior = (lax.rem(row + mix(y, 2, owners - 2), owners), rep)
     partners = (to_y, to_z, to_x, to_core, to_across, to_next, to_prior)
@@ -330,13 +331,12 @@
         load.start()
 
     sends = (
-        (to_y, at(1 - w, 0, 1 - y)),
-        (to_x, at(1 - w, 1, 1 - x)),
+        (to_y, at(1 - w, 1 - u, 1 - y)),
+        (to_y, at(1 - w, u, 1 - y)),
         (to_z, at(w, 1 - u, 1 - y)),
         (to_z, at(w, 1 - u, y)),
     )
-    owns = (at(1 - w, 0, y), at(1 - w, 1, x), at(w, u, 1 - y), row)
-    bits = (x, y, x, x)
+    owns = (at(1 - w, 1 - u, y), at(1 - w, u, y), at(w, u, 1 - y), row)
     mine = core * quad
     theirs = (1 - core) * quad
 
@@ -359,8 +359,7 @@
         return remote(total.at[theirs + n], qrecv.at[n], qs.at[n], qr.at[n], to_core)
 
     def g_copy(i, m):
-        where = (to_x, to_y)[i]
-        return remote(gsend.at[i, m], grecv.at[i, m], gs.at[i, m], gr.at[i, m], where)
+        return remote(gsend.at[i, m], grecv.at[i, m], gs.at[i, m], gr.at[i, m], to_x)
 
     def y_copy(n):
         return remote(ysend.at[n], yrecv.at[n], ys.at[n], yr.at[n], to_y)
@@ -383,18 +382,42 @@
         spot = pair * SPLIT + n
         return remote(block, block, os.at[spot], orr.at[spot], to_core)
 
+    def note(b, held):
+        listed, counts = held[:owners], held[owners:]
+        target = owner_of[b]
+        hits = [target == o for o in range(owners)]
+        return (
+            *[jnp.where(hit, old * blocks + b, old) for hit, old in zip(hits, listed)],
+            *[jnp.where(hit, old + 1, old) for hit, old in zip(hits, counts)],
+        )
+
+    noted = (jnp.int32(0),) * (2 * owners)
+    for b in range(blocks):
+        noted = note(b, noted)
+
+    def slots_for(owner):
+        listed, count = noted[0], noted[owners]
+        for o in range(1, owners):
+            listed = jnp.where(owner == o, noted[o], listed)
+            count = jnp.where(owner == o, noted[owners + o], count)
+        found = []
+        for j in range(most):
+            found.append((listed & (blocks - 1), j < count))
+            listed = listed >> bits_of
+        return found
+
     def pack_v(owner, put):
         lines = lax.broadcasted_iota(jnp.int32, (pad, width), 0)
         marks = jnp.full((pad, width), clusters, jnp.int32)
-        for j in range(most):
-            put(pl.ds(j * rank, rank), vt[tab[0, owner * most + j]])
-            label = tab[1, owner * most + j]
+        for j, (block, valid) in enumerate(slots_for(owner)):
+            put(pl.ds(j * rank, rank), vt[block])
+            label = jnp.where(valid, colc[block], clusters)
             marks = jnp.where(lines == j, label, marks)
         put(pl.ds(depth, pad), marks.astype(F32).astype(BF16))
 
     def pack_c(owner, put):
-        for j in range(most):
-            put(pl.ds(j * rank, rank), cnat[tab[0, owner * most + j]])
+        for j, (block, _) in enumerate(slots_for(owner)):
+            put(pl.ds(j * rank, rank), cnat[block])
 
     def send_v(i):
         def put(spot, value):
@@ -422,8 +445,7 @@
     for load in loads[1:]:
         load.wait()
     pl.semaphore_wait(barrier, len(partners))
-    for i in range(2):
-        v_copy(i).start()
+    v_copy(0).start()
     for copy in halos:
         copy.start()
     v_copy(2).start()
@@ -438,10 +460,11 @@
         for e in range(4):
             coefficients(b * 4 + e)
 
-    for i in range(3):
+    for i in (0, 2):
         send_c(i)
-    v_copy(3).start()
-    send_c(3)
+    for i in (1, 3):
+        v_copy(i).start()
+        send_c(i)
 
     def cut(value):
         return [value[s * sub:(s + 1) * sub] for s in range(SPLIT)]
@@ -468,13 +491,13 @@
 
         pack_v(owns[i], put_v)
         pack_c(owns[i], put_c)
-        prepare(3, vown)
+        prepare(2, vown)
 
         @pl.loop(0, clusters // 2)
         def _(k):
             for e in range(2):
                 c = 2 * k + e
-                for s, value in enumerate(cut(part_of(3, cown, c))):
+                for s, value in enumerate(cut(part_of(2, cown, c))):
                     if i < 3:
                         acc[i, c * SPLIT + s] = value
                     else:
@@ -505,13 +528,13 @@
         raise_acc(y * last, close((1 - y) * last, (1 - y) * 2))
         raise_acc((1 - y) * last, dot_rows(hnear[...], hfield[...]))
 
-    def turn(i, k):
-        side = mix(k // pair, 1 - bits[i], bits[i])
+    def turn(k):
+        side = mix(k // pair, 1 - x, x)
         return side * pair + lax.rem(k, pair)
 
     def ready(i):
         v_copy(i).wait_recv()
-        prepare(min(i, 2), vrecv.at[i])
+        prepare(SPOTS[i], vrecv.at[i])
 
     def partial_away(i):
         c_copy(i).wait_recv()
@@ -519,9 +542,9 @@
         @pl.loop(0, quad // 2)
         def _(k):
             for e in range(2):
-                n = turn(i, 2 * k + e)
+                n = turn(2 * k + e)
                 c = theirs + n
-                value = part_of(min(i, 2), crecv.at[i], c)
+                value = part_of(SPOTS[i], crecv.at[i], c)
                 if i < 3:
                     for s, piece in enumerate(cut(value)):
                         ksend[i, n, s] = (acc[i, c * SPLIT + s] + piece).astype(BF16)
@@ -534,8 +557,8 @@
         @pl.loop(0, count // 2)
         def _(k):
             for e in range(2):
-                c = mine + turn(i, first + 2 * k + e)
-                value = part_of(min(i, 2), crecv.at[i], c)
+                c = mine + turn(first + 2 * k + e)
+                value = part_of(SPOTS[i], crecv.at[i], c)
                 if i < 3:
                     for s, piece in enumerate(cut(value)):
                         acc[i, c * SPLIT + s] = acc[i, c * SPLIT + s] + piece
@@ -550,7 +573,7 @@
 
         @pl.loop(0, pair)
         def _(m):
-            n = (1 - bits[i]) * pair + m
+            n = (1 - x) * pair + m
             k_copy(i, n).wait_recv()
             for s in range(SPLIT):
                 gsend[i, m * SPLIT + s] = summed(i, n, s).astype(BF16)
@@ -559,7 +582,7 @@
     def give_y():
         @pl.loop(0, quad)
         def _(k):
-            n = turn(2, k)
+            n = turn(k)
             k_copy(2, n).wait_recv()
             for s in range(SPLIT):
                 ysend[n, s] = summed(2, n, s).astype(BF16)
@@ -568,26 +591,22 @@
     def take_k(i):
         @pl.loop(0, pair)
         def _(m):
-            k_copy(i, bits[i] * pair + m).wait_recv()
-
-    def reduced(t, m, s):
-        return acc[t, (mine + mix(t, x, y) * pair + m) * SPLIT + s]
+            k_copy(i, x * pair + m).wait_recv()
+
+    def reduced(i, m, s):
+        g_copy(i, m * SPLIT + s).wait_recv()
+        return summed(i, x * pair + m, s) + grecv[i, m * SPLIT + s].astype(F32)
 
     def pass_z(m):
         for s in range(SPLIT):
-            for i in range(2):
-                g_copy(i, m * SPLIT + s).wait_recv()
-                n = bits[i] * pair + m
-                value = summed(i, n, s) + grecv[i, m * SPLIT + s].astype(F32)
-                acc[i, (mine + n) * SPLIT + s] = value
-            zsend[m * SPLIT + s] = reduced(1 - u, m, s).astype(BF16)
+            zsend[m * SPLIT + s] = reduced(0, m, s).astype(BF16)
             z_copy(m * SPLIT + s).start()
 
     def pass_x(m):
         for s in range(SPLIT):
+            value = reduced(1, m, s)
             z_copy(m * SPLIT + s).wait_recv()
-            value = reduced(u, m, s) + zrecv[m * SPLIT + s].astype(F32)
-            xsend[m * SPLIT + s] = value.astype(BF16)
+            xsend[m * SPLIT + s] = (value + zrecv[m * SPLIT + s].astype(F32)).astype(BF16)
             x_copy(m * SPLIT + s).start()
 
     def gathered(n, s):
@@ -601,36 +620,37 @@
             fsend[m * SPLIT + s] = gathered(n, s).astype(BF16)
             f_copy(m * SPLIT + s).start()
 
-    for i in (1, 0, 2):
+    for i in (0, 2):
         own(i)
-    ready(1)
     ready(0)
+    own(1)
     own(3)
     ready(2)
-    partial_away(1)
     partial_away(0)
-    give_g(1)
     give_g(0)
     halo_terms()
     partial_away(2)
     partial_keep(2, 0, quad)
+    partial_keep(0, pair, pair)
     give_y()
-    partial_keep(1, pair, pair)
-    partial_keep(0, pair, pair)
-    take_k(1)
     take_k(0)
     near_field()
     pass_z(0)
+    ready(1)
+    partial_away(1)
+    give_g(1)
+    for m in range(1, pair):
+        pass_z(m)
+    partial_keep(1, pair, pair)
+    take_k(1)
     ready(3)
     partial_away(3)
-    for m in range(1, pair):
-        pass_z(m)
     partial_keep(3, 0, quad)
 
     @pl.loop(0, pair)
     def _(m):
+        pass_f(m)
         pass_x(m)
-        pass_f(m)
 
     @pl.loop(0, pair)
     def _(m):
@@ -724,6 +744,7 @@
         near_blocks,
     )
     cubic = stages == 2 and owners == 2 ** 3 and (blocks - 1).bit_length() * most < 32
+    cubic = cubic and blocks == 2 ** (blocks - 1).bit_length()
     cubic = cubic and columns <= width
     if cubic:
         quad, pair = clusters // 2, clusters // 4
@@ -732,7 +753,7 @@
         gathered = pl.pallas_call(
             functools.partial(cube, most),
             out_shape=jax.ShapeDtypeStruct((clusters * SPLIT, *slab), BF16),
-            in_specs=[smem] * 3 + [pl.BlockSpec(memory_space=pl.ANY)] * 4,
+            in_specs=[smem] * 4 + [pl.BlockSpec(memory_space=pl.ANY)] * 4,
             out_specs=vmem,
             scratch_shapes=[
                 *[keep(array.shape, BF16) for array in arrays],
@@ -743,8 +764,8 @@
                 keep((4, depth, columns), BF16),
                 keep((tall, width), BF16),
                 keep((depth, columns), BF16),
-                keep((4, width, depth), BF16),
-                keep((4, depth, columns), BF16),
+                keep((3, width, depth), BF16),
+                keep((3, depth, columns), BF16),
                 keep((share, width), BF16),
                 keep((share, columns), BF16),
                 keep((clusters, SPLIT, *slab), F32),
@@ -768,7 +789,7 @@
             compiler_params=pltpu.CompilerParams(
                 collective_id=0, has_side_effects=True, vmem_limit_bytes=60 * 1024 * 1024
             ),
-        )(row_cluster, block_ranks, table(slots_of(col_owner, owners, most), clusters, [jnp.arange(blocks, dtype=jnp.int32), col_cluster - clusters]), *arrays)
+        )(row_cluster, block_ranks, col_owner[:, 0], col_cluster, *arrays)
         return gathered.reshape(field_in.shape).astype(F32)
 
     held = slots_of(col_owner, owners, most)

time: 71.7 us -> 67.5 us (0.941)
  the two profiles are of different devices: /device:TPU:9 before, /device:TPU:0 now
where the time goes in v3:
time: 67.5 us; the launch traced here: 67.3 us
  Pallas kernels  64 us (95%)
  other arithmetic  3.36 us (5%)
    pallas_call x1, Pallas kernels, shards(): pl.pallas_call(functools.partial(cube, most), out_shape=jax.ShapeDtypeStr...  64 us
    convert_element_type x1, other arithmetic, shards(): return gathered.reshape(field_in.shape).astype(F32)  3.36 us

profile of v3, /device:TPU:0, one launch (start us, length us, event | category | flops | bytes accessed | tf_op | source)
XLA Modules:
  0.0 67.3 jit_solution(10289388937012914502)
XLA Ops:
  0.0 64.0 %shard_map.82 = bf16[16,192,256]{2,1,0:T(8,128)(2,1)} custom-call(s32[32]{0:T(128)} %rowc.1, s32[32]{0:T(128)} %ranks.1, s32[32]{0:T(128)} %bitcast.10, s32[32]{0:T(128)} %colc.1, bf16[8,384,256]{2,1,0:T(8,128)(2,1)} %field_hbm.1, bf16[32,64,384]{2,1,0:T(8,128)(2,1)} %bitcast.8, bf16[32,64,384]{2,1,0:T(8,128)(2,1)} %bitcast.9, bf16[8,3,96,384]{3,2,1,0:T(8,128)(2,1)} %near_hbm.1), custom_call_target="tpu_custom_call" | custom-call | tf_op jit(solution)/shard_map/pallas_call | solution.py:753
  64.0 3.4 %bitcast_convert_fusion = f32[8,384,256]{2,1,0:T(8,128)} fusion(bf16[8,384,256]{2,1,0:T(8,128)(2,1)} %bitcast.7), kind=kLoop, calls=%fused_computation | loop fusion | flops 786432 | bytes 4718592 | tf_op jit(solution)/shard_map/convert_element_type | solution.py:793

commit v4 on v3

--- a/solution.py
+++ b/solution.py
@@ -280,8 +280,8 @@
 
 
 def cube(
-    most, rowc, ranks, owner_of, colc, field_hbm, ut_hbm, vt_hbm, near_hbm, out,
-    field, ut, vt, near,
+    most, facts_hbm, field_hbm, ut_hbm, vt_hbm, near_hbm, out,
+    facts, field, ut, vt, near,
     cnat, vsend, csend, vrecv, crecv, vown, cown, vtr, labels, hnear, hfield, total, acc,
     ksend, krecv, qrecv, gsend, grecv, ysend, yrecv, zsend, zrecv,
     xsend, xrecv, fsend, frecv,
@@ -324,7 +324,10 @@
     loads = [
         pltpu.make_async_copy(src, dst, ins.at[i])
         for i, (src, dst) in enumerate(
-            ((vt_hbm, vt), (ut_hbm, ut), (field_hbm, field), (near_hbm, near))
+            (
+                (facts_hbm, facts), (vt_hbm, vt), (ut_hbm, ut),
+                (field_hbm, field), (near_hbm, near),
+            )
         )
     ]
     for load in loads:
@@ -384,13 +387,14 @@
 
     def note(b, held):
         listed, counts = held[:owners], held[owners:]
-        target = owner_of[b]
+        target = facts[0, b]
         hits = [target == o for o in range(owners)]
         return (
             *[jnp.where(hit, old * blocks + b, old) for hit, old in zip(hits, listed)],
             *[jnp.where(hit, old + 1, old) for hit, old in zip(hits, counts)],
         )
 
+    loads[0].wait()
     noted = (jnp.int32(0),) * (2 * owners)
     for b in range(blocks):
         noted = note(b, noted)
@@ -411,7 +415,7 @@
         marks = jnp.full((pad, width), clusters, jnp.int32)
         for j, (block, valid) in enumerate(slots_for(owner)):
             put(pl.ds(j * rank, rank), vt[block])
-            label = jnp.where(valid, colc[block], clusters)
+            label = jnp.where(valid, facts[1, block], clusters)
             marks = jnp.where(lines == j, label, marks)
         put(pl.ds(depth, pad), marks.astype(F32).astype(BF16))
 
@@ -439,10 +443,10 @@
         remote(field.at[y * last, my_rows, :], hfield, hs.at[1], hr.at[1], to_next),
     ]
 
-    loads[0].wait()
+    loads[1].wait()
     for i in range(4):
         send_v(i)
-    for load in loads[1:]:
+    for load in loads[2:]:
         load.wait()
     pl.semaphore_wait(barrier, len(partners))
     v_copy(0).start()
@@ -451,8 +455,8 @@
     v_copy(2).start()
 
     def coefficients(b):
-        value = jnp.dot(ut[b], field[rowc[b]], preferred_element_type=F32)
-        kept = lax.broadcasted_iota(jnp.int32, (rank, columns), 0) < ranks[b]
+        value = jnp.dot(ut[b], field[facts[2, b]], preferred_element_type=F32)
+        kept = lax.broadcasted_iota(jnp.int32, (rank, columns), 0) < facts[3, b]
         cnat[b] = jnp.where(kept, value, 0.0).astype(BF16)
 
     @pl.loop(0, blocks // 4)
@@ -753,9 +757,10 @@
         gathered = pl.pallas_call(
             functools.partial(cube, most),
             out_shape=jax.ShapeDtypeStruct((clusters * SPLIT, *slab), BF16),
-            in_specs=[smem] * 4 + [pl.BlockSpec(memory_space=pl.ANY)] * 4,
+            in_specs=[pl.BlockSpec(memory_space=pltpu.HBM)] * 5,
             out_specs=vmem,
             scratch_shapes=[
+                pltpu.SMEM((4, blocks), jnp.int32),
                 *[keep(array.shape, BF16) for array in arrays],
                 keep((blocks, rank, columns), BF16),
                 keep((4, tall, width), BF16),
@@ -778,7 +783,8 @@
                 keep((quad, SPLIT, *slab), BF16),
                 keep((quad, SPLIT, *slab), BF16),
                 *[keep((pair * SPLIT, *slab), BF16)] * 6,
-                *[dma((4,))] * 7,
+                dma((5,)),
+                *[dma((4,))] * 6,
                 *[dma((3, quad))] * 2,
                 *[dma((quad,))] * 2,
                 *[dma((2, pair * SPLIT))] * 2,
@@ -787,9 +793,9 @@
                 *[dma(((pair + quad) * SPLIT,))] * 2,
             ],
             compiler_params=pltpu.CompilerParams(
-                collective_id=0, has_side_effects=True, vmem_limit_bytes=60 * 1024 * 1024
+                collective_id=0, has_side_effects=True, vmem_limit_bytes=52 * 1024 * 1024
             ),
-        )(row_cluster, block_ranks, col_owner[:, 0], col_cluster, *arrays)
+        )(jnp.stack([col_owner[:, 0], col_cluster, row_cluster, block_ranks]), *arrays)
         return gathered.reshape(field_in.shape).astype(F32)
 
     held = slots_of(col_owner, owners, most)

time: 67.5 us -> 64.8 us (0.960)
  Pallas kernels: 64 us -> 62 us
  other arithmetic: 3.36 us -> 2.67 us
    pallas_call x1, Pallas kernels: 64 us -> 62 us  [shards(): pl.pallas_call(functools.partial(cube, most), out_shape=jax.ShapeDtypeStr...]
    convert_element_type x1, other arithmetic: 3.36 us -> 1.95 us  [shards(): return gathered.reshape(field_in.shape).astype(F32)]
    another operation x0 -> x1, other arithmetic: none -> 0.71 us  [shards(): jnp.stack([col_owner[:, 0], col_cluster, row_cluster, block_ranks])]
where the time goes in v4:
time: 64.8 us; the launch traced here: 64.7 us
  Pallas kernels  62 us (96%)
  other arithmetic  2.67 us (4%)
    pallas_call x1, Pallas kernels, shards(): pl.pallas_call(functools.partial(cube, most), out_shape=jax.ShapeDtypeStr...  62 us
    convert_element_type x1, other arithmetic, shards(): return gathered.reshape(field_in.shape).astype(F32)  1.95 us

profile of v4, /device:TPU:0, one launch (start us, length us, event | category | flops | bytes accessed | tf_op | source)
XLA Modules:
  0.0 64.7 jit_solution(9955081933759213020)
XLA Ops:
  0.0 0.7 %pad_add_fusion.facts_hbm = s32[4,32]{1,0:T(4,128)S(1)} fusion(s32[1,32]{1,0:T(1,128)} %bitcast.13, s32[1,32]{1,0:T(1,128)} %bitcast.14, s32[1,32]{1,0:T(1,128)} %bitcast.15, s32[1,32]{1,0:T(1,128)} %bitcast.16), kind=kLoop, calls=%fused_computation.1 | loop fusion | flops 384 | bytes 1024 | tf_op jit(solution)/shard_map/stack | solution.py:798
  0.7 62.0 %shard_map.82 = bf16[16,192,256]{2,1,0:T(8,128)(2,1)S(1)} custom-call(s32[4,32]{1,0:T(4,128)S(1)} %pad_add_fusion.facts_hbm, bf16[8,384,256]{2,1,0:T(8,128)(2,1)} %field_hbm.1, bf16[32,64,384]{2,1,0:T(8,128)(2,1)} %bitcast.11, bf16[32,64,384]{2,1,0:T(8,128)(2,1)} %bitcast.12, bf16[8,3,96,384]{3,2,1,0:T(8,128)(2,1)} %near_hbm.1), custom_call_target="tpu_custom_call" | custom-call | tf_op jit(solution)/shard_map/pallas_call | solution.py:757
  62.7 2.0 %bitcast_convert_fusion = f32[8,384,256]{2,1,0:T(8,128)} fusion(bf16[8,384,256]{2,1,0:T(8,128)(2,1)S(1)} %bitcast.10), kind=kLoop, calls=%fused_computation | loop fusion | flops 786432 | bytes 4718592 | tf_op jit(solution)/shard_map/convert_element_type | solution.py:799

commit v5 on v4

--- a/solution.py
+++ b/solution.py
@@ -330,7 +330,7 @@
             )
         )
     ]
-    for load in loads:
+    for load in loads[:2]:
         load.start()
 
     sends = (
@@ -444,15 +444,19 @@
     ]
 
     loads[1].wait()
-    for i in range(4):
+    for load in loads[2:]:
+        load.start()
+    send_v(0)
+    pl.semaphore_wait(barrier, len(partners))
+    v_copy(0).start()
+    send_v(2)
+    v_copy(2).start()
+    for i in (1, 3):
         send_v(i)
     for load in loads[2:]:
         load.wait()
-    pl.semaphore_wait(barrier, len(partners))
-    v_copy(0).start()
     for copy in halos:
         copy.start()
-    v_copy(2).start()
 
     def coefficients(b):
         value = jnp.dot(ut[b], field[facts[2, b]], preferred_element_type=F32)
@@ -540,21 +544,22 @@
         v_copy(i).wait_recv()
         prepare(SPOTS[i], vrecv.at[i])
 
-    def partial_away(i):
-        c_copy(i).wait_recv()
-
-        @pl.loop(0, quad // 2)
+    def partial_away(i, first, count):
+        @pl.loop(0, count // 2)
         def _(k):
-            for e in range(2):
-                n = turn(2 * k + e)
+            spots = [turn(first + 2 * k + e) for e in range(2)]
+            for n in spots:
                 c = theirs + n
                 value = part_of(SPOTS[i], crecv.at[i], c)
                 if i < 3:
                     for s, piece in enumerate(cut(value)):
                         ksend[i, n, s] = (acc[i, c * SPLIT + s] + piece).astype(BF16)
+                else:
+                    raise_total(c, value)
+            for n in spots:
+                if i < 3:
                     k_copy(i, n).start()
                 else:
-                    raise_total(c, value)
                     q_copy(n).start()
 
     def partial_keep(i, first, count):
@@ -630,10 +635,13 @@
     own(1)
     own(3)
     ready(2)
-    partial_away(0)
+    c_copy(0).wait_recv()
+    partial_away(0, 0, pair)
     give_g(0)
+    partial_away(0, pair, pair)
     halo_terms()
-    partial_away(2)
+    c_copy(2).wait_recv()
+    partial_away(2, 0, quad)
     partial_keep(2, 0, quad)
     partial_keep(0, pair, pair)
     give_y()
@@ -641,14 +649,17 @@
     near_field()
     pass_z(0)
     ready(1)
-    partial_away(1)
+    c_copy(1).wait_recv()
+    partial_away(1, 0, pair)
     give_g(1)
+    partial_away(1, pair, pair)
     for m in range(1, pair):
         pass_z(m)
     partial_keep(1, pair, pair)
     take_k(1)
     ready(3)
-    partial_away(3)
+    c_copy(3).wait_recv()
+    partial_away(3, 0, quad)
     partial_keep(3, 0, quad)
 
     @pl.loop(0, pair)

time: 64.8 us -> 63.9 us (0.986)
  Pallas kernels: 62 us -> 61.1 us
    pallas_call x1, Pallas kernels: 62 us -> 61.1 us  [shards(): pl.pallas_call(functools.partial(cube, most), out_shape=jax.ShapeDtypeStr...]
where the time goes in v5:
time: 63.9 us; the launch traced here: 63.8 us
  Pallas kernels  61.1 us (96%)
  other arithmetic  2.67 us (4%)
    pallas_call x1, Pallas kernels, shards(): pl.pallas_call(functools.partial(cube, most), out_shape=jax.ShapeDtypeStr...  61.1 us
    convert_element_type x1, other arithmetic, shards(): return gathered.reshape(field_in.shape).astype(F32)  1.95 us

profile of v5, /device:TPU:0, one launch (start us, length us, event | category | flops | bytes accessed | tf_op | source)
XLA Modules:
  0.0 63.8 jit_solution(13971376800156876961)
XLA Ops:
  0.0 0.7 %pad_add_fusion.facts_hbm = s32[4,32]{1,0:T(4,128)S(1)} fusion(s32[1,32]{1,0:T(1,128)} %bitcast.13, s32[1,32]{1,0:T(1,128)} %bitcast.14, s32[1,32]{1,0:T(1,128)} %bitcast.15, s32[1,32]{1,0:T(1,128)} %bitcast.16), kind=kLoop, calls=%fused_computation.1 | loop fusion | flops 384 | bytes 1024 | tf_op jit(solution)/shard_map/stack | solution.py:809
  0.7 61.1 %shard_map.82 = bf16[16,192,256]{2,1,0:T(8,128)(2,1)S(1)} custom-call(s32[4,32]{1,0:T(4,128)S(1)} %pad_add_fusion.facts_hbm, bf16[8,384,256]{2,1,0:T(8,128)(2,1)} %field_hbm.1, bf16[32,64,384]{2,1,0:T(8,128)(2,1)} %bitcast.11, bf16[32,64,384]{2,1,0:T(8,128)(2,1)} %bitcast.12, bf16[8,3,96,384]{3,2,1,0:T(8,128)(2,1)} %near_hbm.1), custom_call_target="tpu_custom_call" | custom-call | tf_op jit(solution)/shard_map/pallas_call | solution.py:768
  61.8 2.0 %bitcast_convert_fusion = f32[8,384,256]{2,1,0:T(8,128)} fusion(bf16[8,384,256]{2,1,0:T(8,128)(2,1)S(1)} %bitcast.10), kind=kLoop, calls=%fused_computation | loop fusion | flops 786432 | bytes 4718592 | tf_op jit(solution)/shard_map/convert_element_type | solution.py:810

commit v6 on v5

--- a/solution.py
+++ b/solution.py
@@ -453,10 +453,8 @@
     v_copy(2).start()
     for i in (1, 3):
         send_v(i)
-    for load in loads[2:]:
+    for load in loads[2:4]:
         load.wait()
-    for copy in halos:
-        copy.start()
 
     def coefficients(b):
         value = jnp.dot(ut[b], field[facts[2, b]], preferred_element_type=F32)
@@ -468,8 +466,11 @@
         for e in range(4):
             coefficients(b * 4 + e)
 
-    for i in (0, 2):
-        send_c(i)
+    send_c(0)
+    loads[4].wait()
+    for copy in halos:
+        copy.start()
+    send_c(2)
     for i in (1, 3):
         v_copy(i).start()
         send_c(i)

time: 63.9 us -> 63.9 us (level)
  no operation moved by 1% of the time
where the time goes in v6:
time: 63.9 us; the launch traced here: 63.8 us
  Pallas kernels  61.1 us (96%)
  other arithmetic  2.67 us (4%)
    pallas_call x1, Pallas kernels, shards(): pl.pallas_call(functools.partial(cube, most), out_shape=jax.ShapeDtypeStr...  61.1 us
    convert_element_type x1, other arithmetic, shards(): return gathered.reshape(field_in.shape).astype(F32)  1.95 us

profile of v6, /device:TPU:0, one launch (start us, length us, event | category | flops | bytes accessed | tf_op | source)
XLA Modules:
  0.0 63.8 jit_solution(16182426642625624231)
XLA Ops:
  0.0 0.7 %pad_add_fusion.facts_hbm = s32[4,32]{1,0:T(4,128)S(1)} fusion(s32[1,32]{1,0:T(1,128)} %bitcast.13, s32[1,32]{1,0:T(1,128)} %bitcast.14, s32[1,32]{1,0:T(1,128)} %bitcast.15, s32[1,32]{1,0:T(1,128)} %bitcast.16), kind=kLoop, calls=%fused_computation.1 | loop fusion | flops 384 | bytes 1024 | tf_op jit(solution)/shard_map/stack | solution.py:810
  0.7 61.1 %shard_map.82 = bf16[16,192,256]{2,1,0:T(8,128)(2,1)S(1)} custom-call(s32[4,32]{1,0:T(4,128)S(1)} %pad_add_fusion.facts_hbm, bf16[8,384,256]{2,1,0:T(8,128)(2,1)} %field_hbm.1, bf16[32,64,384]{2,1,0:T(8,128)(2,1)} %bitcast.11, bf16[32,64,384]{2,1,0:T(8,128)(2,1)} %bitcast.12, bf16[8,3,96,384]{3,2,1,0:T(8,128)(2,1)} %near_hbm.1), custom_call_target="tpu_custom_call" | custom-call | tf_op jit(solution)/shard_map/pallas_call | solution.py:769
  61.8 2.0 %bitcast_convert_fusion = f32[8,384,256]{2,1,0:T(8,128)} fusion(bf16[8,384,256]{2,1,0:T(8,128)(2,1)S(1)} %bitcast.10), kind=kLoop, calls=%fused_computation | loop fusion | flops 786432 | bytes 4718592 | tf_op jit(solution)/shard_map/convert_element_type | solution.py:811
